TPU v7x, 32 devices: a whole 2x2x4 slice. The times are simulated.
32 devices in a mesh: fourier: 2 (over x), ex: 4 (over z), ey: 4 (over y, core).
Axes of the slice: x: 2, y: 2, z: 4, core: 2. Of those that a mesh axis runs over, the one named last changes fastest.
Arguments:
- forcing: float32 [128, 81, 2048], P('fourier', None, ('ex', 'ey')), may hold values from -6 to 6
- element_coef: float32 [2048], P(('ex', 'ey')), may hold values from 0.5 to 2
- schur: float32 [128, 32, 32], P('fourier'), may hold values from -12 to 20, as said below
- couple: float32 [128, 32, 49], P('fourier'), may hold values from -0.875 to 0.875
- inner_inv: float32 [128, 49, 49], P('fourier'), may hold values from -3 to 4.5, as said below
- element_cell: int32 [2048], P(('ex', 'ey')), may hold values from 0 to 127, as said below
Outputs:
- velocity: float32 [128, 81, 2048], P('fourier', None, ('ex', 'ey'))
Inputs may be any that keep to these rules, and one draw needn't show every extreme that they name: `element_cell`: each aligned block of 128 entries is a permutation of 0 to 127. `schur`: each matrix is symmetric positive definite. `inner_inv`: each matrix is symmetric positive definite.
All inputs are finite; a program needn't handle non-finite values.
Results may differ from a plain program's by a relative error of at most 0.0001.
Values sent between devices are 32-bit elements; how exact they have to be, the bound alone decides.
A program may use at most 128 MiB of HBM per device.

v0:
```python
import functools
import math

import jax
import jax.numpy as jnp
import numpy as np
from jax import lax
from jax.experimental import pallas as pl
from jax.experimental.pallas import tpu as pltpu
from jax.sharding import PartitionSpec as P

P_SIZE = 8
ITERS = 3
ELX = 8
ELY = 16
NB = 4 * P_SIZE
HIGH = lax.Precision.HIGH
HIGHEST = lax.Precision.HIGHEST


def dft_rows(length):
    row_index = jnp.arange(length)[:, None]
    plane_pos = jnp.arange(length, dtype=jnp.float32)[None, :]
    waves = ((row_index + 1) // 2).astype(jnp.float32)
    angles = 2.0 * math.pi * waves * plane_pos / length
    factor = math.sqrt(2.0 / length)
    result = jnp.where(row_index % 2 == 1, factor * jnp.cos(angles), factor * jnp.sin(angles))
    result = jnp.where(row_index == 0, 1.0 / math.sqrt(length), result)
    result = jnp.where(
        row_index == length - 1, jnp.cos(math.pi * plane_pos) / math.sqrt(length), result
    )
    return result


def node_masks():
    slots = np.arange(NB)[:, None]
    cells = jnp.arange(ELX * ELY)[None, :]
    row_ids = lax.axis_index("ex") * ELX + cells // ELY
    col_ids = lax.axis_index("ey") * ELY + cells % ELY
    rows_total = ELX * lax.axis_size("ex")
    cols_total = ELY * lax.axis_size("ey")
    on_left = jnp.asarray((slots == 0) | (slots >= 3 * P_SIZE))
    on_right = jnp.asarray((slots >= P_SIZE) & (slots <= 2 * P_SIZE))
    on_bottom = jnp.asarray(slots <= P_SIZE)
    on_top = jnp.asarray((slots >= 2 * P_SIZE) & (slots <= 3 * P_SIZE))
    dropped = (
        on_left & (row_ids == 0)
        | on_right & (row_ids == rows_total - 1)
        | on_bottom & (col_ids == 0)
        | on_top & (col_ids == cols_total - 1)
    )
    keep = jnp.where(dropped, 0.0, 1.0).astype(jnp.float32)
    corner_weight = jnp.asarray(np.where(slots % P_SIZE == 0, 0.25, 0.5).astype(np.float32))
    return keep, keep * corner_weight


def split_high_low(values):
    high = lax.reduce_precision(values, 8, 7)
    return high.astype(jnp.bfloat16), (values - high).astype(jnp.bfloat16)


def cg_kernel(
    modes,
    cond_ref,
    schur_ref,
    scale_ref,
    keep_ref,
    weight_ref,
    x_ref,
    res_ref,
    app_ref,
    dir_ref,
    along_ref,
    xs_ref,
    xr_ref,
    ys_ref,
    yr_ref,
    ps_ref,
    pr_ex,
    pr_ey,
    halo_send,
    halo_recv,
    sum_send_ex,
    sum_recv_ex,
    sum_send_ey,
    sum_recv_ey,
):
    cells = cond_ref.shape[1]
    sizes = {axis: lax.axis_size(axis) for axis in ("ex", "ey")}
    place = {axis: lax.axis_index(axis) for axis in ("ex", "ey")}
    lane = lax.broadcasted_iota(jnp.int32, (modes, cells), 1)
    lane_row = lane // ELY
    lane_col = lane % ELY

    def node(n):
        if isinstance(n, int):
            return pl.ds(n * modes, modes)
        return pl.ds(pl.multiple_of(n * modes, modes), modes)

    def turned(value, shift):
        shift = shift % cells
        return pltpu.roll(value, shift, 1) if shift else value

    xr_ref[...] = jnp.zeros_like(xr_ref)
    yr_ref[...] = jnp.zeros_like(yr_ref)

    barrier = pltpu.get_barrier_semaphore()
    for axis in ("ex", "ey"):
        for hop in range(1, sizes[axis]):
            pl.semaphore_signal(
                barrier,
                inc=1,
                device_id={axis: lax.rem(place[axis] + hop, sizes[axis])},
                device_id_type=pl.DeviceIdType.MESH,
            )
    for ex_step in (1, -1):
        for ey_step in (1, -1):
            pl.semaphore_signal(
                barrier,
                inc=1,
                device_id={
                    "ex": lax.rem(place["ex"] + ex_step + sizes["ex"], sizes["ex"]),
                    "ey": lax.rem(place["ey"] + ey_step + sizes["ey"], sizes["ey"]),
                },
                device_id_type=pl.DeviceIdType.MESH,
            )
    pl.semaphore_wait(barrier, sizes["ex"] + sizes["ey"] + 2)

    def exists(axis, step):
        if step == 0:
            return None
        return place[axis] < sizes[axis] - 1 if step > 0 else place[axis] > 0

    def guarded(ex_step, ey_step, action):
        tests = [t for t in (exists("ex", ex_step), exists("ey", ey_step)) if t is not None]
        pl.when(functools.reduce(jnp.logical_and, tests))(action)

    def halo_copy(turn, number, source, target, ex_step, ey_step):
        copy = pltpu.make_async_remote_copy(
            src_ref=source,
            dst_ref=target,
            send_sem=halo_send.at[turn, number],
            recv_sem=halo_recv.at[turn, number],
            device_id={
                "ex": lax.rem(place["ex"] + ex_step + sizes["ex"], sizes["ex"]),
                "ey": lax.rem(place["ey"] + ey_step + sizes["ey"], sizes["ey"]),
            },
            device_id_type=pl.DeviceIdType.MESH,
        )
        guarded(ex_step, ey_step, copy.start)

        def arrive():
            guarded(-ex_step, -ey_step, copy.wait_recv)

        def leave():
            guarded(ex_step, ey_step, copy.wait_send)

        return arrive, leave

    def assemble(ref, turn):
        bottom = lambda k: k
        top = lambda k: 3 * P_SIZE - k
        up = jnp.zeros((modes, cells), jnp.float32)
        down = up
        for k in range(P_SIZE + 1):
            up = jnp.where(lane_col == k, turned(ref[node(top(k)), :], k - ELY + 1), up)
            down = jnp.where(lane_col == k, turned(ref[node(bottom(k)), :], k), down)
        ys_ref[turn, 0] = up
        ys_ref[turn, 1] = down
        copies = []
        for slot, ex_step in ((1, 1), (2, -1), (0, 0)):
            for way, ey_step in ((0, 1), (1, -1)):
                copies.append(
                    halo_copy(
                        turn,
                        2 * slot + way,
                        ys_ref.at[turn, way],
                        yr_ref.at[turn, slot, way],
                        ex_step,
                        ey_step,
                    )
                )

        left = lambda k: (NB - k) % NB
        right = lambda k: P_SIZE + k
        last = cells - ELY
        up = jnp.zeros((modes, cells), jnp.float32)
        down = up
        for k in range(P_SIZE):
            up = jnp.where(lane_row == k, turned(ref[node(right(k)), :], ELY * k - last), up)
            down = jnp.where(lane_row == k, turned(ref[node(left(k)), :], ELY * k), down)
        xs_ref[turn, 0, 0] = up
        xs_ref[turn, 1, 0] = down
        xs_ref[turn, 0, 1] = turned(ref[node(right(P_SIZE)), :], -last)
        xs_ref[turn, 1, 1] = ref[node(left(P_SIZE)), :]
        for way, ex_step in ((0, 1), (1, -1)):
            copies.append(
                halo_copy(turn, 6 + way, xs_ref.at[turn, way], xr_ref.at[turn, way], ex_step, 0)
            )

        for k in range(P_SIZE + 1):
            here_left, here_right = ref[node(left(k)), :], ref[node(right(k)), :]
            ref[node(left(k)), :] = here_left + jnp.where(
                lane_row == 0, 0.0, turned(here_right, ELY)
            )
            ref[node(right(k)), :] = here_right + jnp.where(
                lane_row == ELX - 1, 0.0, turned(here_left, -ELY)
            )
        for arrive, _ in copies:
            arrive()

        for k in range(P_SIZE + 1):
            part, lanes = divmod(k, P_SIZE)
            low = turned(xr_ref[turn, 0, part], -ELY * lanes)
            high = turned(xr_ref[turn, 1, part], last - ELY * lanes)
            for n, halo, row in ((left(k), low, 0), (right(k), high, ELX - 1)):
                value = ref[node(n), :] + jnp.where(lane_row == row, halo, 0.0)
                if n % (2 * P_SIZE) > P_SIZE:
                    value = value * keep_ref[n : n + 1, :]
                ref[node(n), :] = value

        lines = []
        for way in range(2):
            line = yr_ref[turn, 0, way]
            before = jnp.where(
                lane == 0, turned(yr_ref[turn, 1, way], P_SIZE), turned(line, P_SIZE)
            )
            after = jnp.where(
                lane == last + P_SIZE, turned(yr_ref[turn, 2, way], -P_SIZE), turned(line, -P_SIZE)
            )
            lines.append(
                line
                + jnp.where(lane_col == 0, before, jnp.where(lane_col == P_SIZE, after, 0.0))
            )
        low_all, high_all = lines
        for k in range(P_SIZE + 1):
            b, t = bottom(k), top(k)
            here_bottom, here_top = ref[node(b), :], ref[node(t), :]
            ref[node(b), :] = keep_ref[b : b + 1, :] * (
                here_bottom
                + jnp.where(lane_col == 0, turned(low_all, -k), turned(here_top, 1))
            )
            ref[node(t), :] = keep_ref[t : t + 1, :] * (
                here_top
                + jnp.where(
                    lane_col == ELY - 1, turned(high_all, ELY - 1 - k), turned(here_bottom, -1)
                )
            )
        for _, leave in copies:
            leave()

    def operator(turn):
        scale = scale_ref[0:1, :]
        block = 8

        def step(outer, carry):
            for inner in range(block):
                mode = outer * block + inner
                value = res_ref[pl.ds(mode, NB, stride=modes), :]
                high = value.astype(jnp.bfloat16)
                low = (value - high.astype(jnp.float32)).astype(jnp.bfloat16)
                image = jnp.dot(
                    schur_ref[mode],
                    jnp.concatenate([high, low, high], 0),
                    preferred_element_type=jnp.float32,
                )
                app_ref[pl.ds(mode, NB, stride=modes), :] = image * scale
            return carry

        lax.fori_loop(0, modes // block, step, 0)
        assemble(app_ref, turn)

    def group_sum(mine, axis, turn, stage, slots, send_sem, recv_sem):
        ps_ref[turn, stage] = mine
        copies = [
            pltpu.make_async_remote_copy(
                src_ref=ps_ref.at[turn, stage],
                dst_ref=slots.at[turn, hop - 1],
                send_sem=send_sem.at[turn, hop - 1],
                recv_sem=recv_sem.at[turn, hop - 1],
                device_id={axis: lax.rem(place[axis] + hop, sizes[axis])},
                device_id_type=pl.DeviceIdType.MESH,
            )
            for hop in range(1, sizes[axis])
        ]
        for copy in copies:
            copy.start()
        for hop, copy in enumerate(copies):
            copy.wait_recv()
            mine = mine + slots[turn, hop]
        for copy in copies:
            copy.wait_send()
        return mine

    def paired(turn):
        def step(n, sums):
            weighted = weight_ref[pl.ds(n, 1), :] * res_ref[node(n), :]
            return (
                sums[0] + weighted * res_ref[node(n), :],
                sums[1] + weighted * app_ref[node(n), :],
            )

        zero = jnp.zeros((modes, cells), jnp.float32)
        norm, curve = lax.fori_loop(0, NB, step, (zero, zero))
        total = lax.dot_general(
            jnp.ones((8, cells), jnp.float32),
            jnp.concatenate([norm, curve], 0),
            (((1,), (1,)), ((), ())),
            precision=HIGHEST,
            preferred_element_type=jnp.float32,
        )
        total = group_sum(total, "ey", turn, 0, pr_ey, sum_send_ey, sum_recv_ey)
        total = group_sum(total, "ex", turn, 1, pr_ex, sum_send_ex, sum_recv_ex)
        row = lax.broadcasted_iota(jnp.int32, (modes, 2 * modes), 0)
        column = lax.broadcasted_iota(jnp.int32, (modes, 2 * modes), 1)
        pick = lambda offset: jnp.sum(
            jnp.where(column == row + offset, total[0:1, :], 0.0), axis=1, keepdims=True
        )
        return pick(0), pick(modes)

    res_ref[...] = cond_ref[...]
    assemble(res_ref, 0)
    for ref in (x_ref, dir_ref, along_ref):
        ref[...] = jnp.zeros_like(ref)

    def sweep(turn, scalars):
        norm_now, step_size = scalars
        operator(turn + 1)
        norm_next, curve_now = paired(turn)
        conj_ratio = jnp.where(turn == 0, 0.0, norm_next / norm_now)
        step_size = norm_next / (curve_now - conj_ratio * norm_next / step_size)

        def update(n, carry):
            rows = node(n)
            search = res_ref[rows, :] + conj_ratio * dir_ref[rows, :]
            along = app_ref[rows, :] + conj_ratio * along_ref[rows, :]
            x_ref[rows, :] = x_ref[rows, :] + step_size * search
            dir_ref[rows, :] = search
            along_ref[rows, :] = along
            res_ref[rows, :] = res_ref[rows, :] - step_size * along
            return carry

        lax.fori_loop(0, NB, update, 0)
        return norm_next, step_size

    one = jnp.ones((modes, 1), jnp.float32)
    lax.fori_loop(0, ITERS, sweep, (one, one))


def conjugate_gradients(condensed, stacked, scaling, keep, weights):
    modes, cells = condensed.shape[1:]
    field = pltpu.VMEM((NB * modes, cells), jnp.float32)
    along_ex, along_ey = lax.axis_size("ex") - 1, lax.axis_size("ey") - 1
    turns = ITERS + 1
    strips = lambda *lead: pltpu.VMEM(lead + (modes, cells), jnp.float32)
    tile = lambda *lead: pltpu.VMEM(lead + (8, 2 * modes), jnp.float32)
    semaphores = lambda *dims: pltpu.SemaphoreType.DMA(dims)
    whole = pl.BlockSpec(memory_space=pltpu.VMEM)
    solved = pl.pallas_call(
        functools.partial(cg_kernel, modes),
        out_shape=jax.ShapeDtypeStruct((NB * modes, cells), jnp.float32),
        in_specs=[whole] * 5,
        out_specs=whole,
        scratch_shapes=[field] * 4
        + [
            strips(turns, 2, 2),
            strips(turns, 2, 2),
            strips(turns, 2),
            strips(turns, 3, 2),
            tile(ITERS, 2),
            tile(ITERS, along_ex),
            tile(ITERS, along_ey),
            semaphores(turns, 8),
            semaphores(turns, 8),
            semaphores(ITERS, along_ex),
            semaphores(ITERS, along_ex),
            semaphores(ITERS, along_ey),
            semaphores(ITERS, along_ey),
        ],
        compiler_params=pltpu.CompilerParams(
            collective_id=0, has_side_effects=True, vmem_limit_bytes=40 << 20
        ),
        cost_estimate=pl.CostEstimate(flops=10**9, bytes_accessed=2 * 10**8, transcendentals=0),
    )(condensed.reshape(NB * modes, cells), stacked, scaling[None], keep, weights)
    return solved.reshape(NB, modes, cells)


def on_device(forcing, element_coef, schur, couple, inner_inv, element_cell):
    modes_dev = schur.shape[0]
    planes_dev = forcing.shape[0]
    elements = forcing.shape[2]
    groups = lax.axis_size("fourier")
    me = lax.axis_index("fourier")
    dft_table = dft_rows(modes_dev * groups)
    swap = [[(i, (i + hop) % groups) for i in range(groups)] for hop in range(groups)]
    plane_of = lambda group: lax.dynamic_slice_in_dim(dft_table, group * planes_dev, planes_dev, 1)
    rows_of = lambda table, group: lax.dynamic_slice_in_dim(table, group * modes_dev, modes_dev, 0)

    own_planes = plane_of(me)
    one_hot = (element_cell[:, None] == jnp.arange(elements)[None, :]).astype(jnp.float32)
    scaling = jnp.einsum("e,ec->c", element_coef, one_hot, precision=HIGHEST)

    order = [(me - hop) % groups for hop in range(groups)]
    middle = couple.shape[1] // 2
    folded = jnp.concatenate([couple[:, :middle], couple[:, middle:]], 0)
    couples = [couple]
    for hop in range(1, groups):
        arrived = lax.ppermute(folded, "fourier", swap[hop])
        couples.append(jnp.concatenate([arrived[:modes_dev], arrived[modes_dev:]], 1))

    partial = []
    condensed = None
    for hop in range(groups):
        spec = jnp.einsum(
            "mz,zne->mne", rows_of(own_planes, order[hop]), forcing, precision=HIGH
        )
        partial.append(spec[:, NB:])
        term = spec[:, :NB] - jnp.einsum("mbi,mie->mbe", couples[hop], spec[:, NB:], precision=HIGH)
        if hop:
            term = lax.ppermute(term, "fourier", [(b, a) for a, b in swap[hop]])
        condensed = term if condensed is None else condensed + term

    half, inner_count = modes_dev // 2, inner_inv.shape[2]
    padded = jnp.pad(inner_inv, ((0, 0), (0, 0), (0, elements // 2 - inner_count)))
    parcel = jnp.concatenate(
        [forcing[:, NB:], jnp.concatenate([padded[:half], padded[half:]], 2)], 0
    )
    keep, weights = node_masks()
    high, low = split_high_low(schur)
    stacked = jnp.concatenate([high, high, low], 2)
    condensed, parcel, stacked, scaling, keep, weights = lax.optimization_barrier(
        (condensed, parcel, stacked, scaling, keep, weights)
    )
    parcels = [None] + [lax.ppermute(parcel, "fourier", swap[h]) for h in range(1, groups)]
    condensed = jnp.einsum("mbe,ec->bmc", condensed, one_hot, precision=HIGH)
    iterate = conjugate_gradients(condensed, stacked, scaling, keep, weights)
    iterate = jnp.einsum("bmc,ec->mbe", iterate, one_hot, precision=HIGH)
    iterate, inner_inv = lax.optimization_barrier((iterate, inner_inv))

    cycles = [iterate] + [lax.ppermute(iterate, "fourier", swap[h]) for h in range(1, groups)]
    bases = []
    for hop in range(groups):
        inverse = inner_inv
        if hop:
            pairs = parcels[hop][planes_dev:]
            inverse = jnp.concatenate(
                [pairs[:, :, :inner_count], pairs[:, :, elements // 2 :][:, :, :inner_count]], 0
            )
        inner = partial[hop]
        for far in range(1, groups):
            inner = inner + jnp.einsum(
                "mz,zne->mne",
                rows_of(plane_of(order[far]), order[hop]),
                parcels[far][:planes_dev],
                precision=HIGH,
            )
        bases.append(jnp.einsum("mij,mje->mie", inverse, inner, precision=HIGH) / element_coef)

    def back(hop, cycle, base):
        interior = base - jnp.einsum("mbi,mbe->mie", couples[hop], cycle, precision=HIGH)
        return jnp.einsum(
            "mz,mne->zne",
            rows_of(own_planes, order[hop]),
            jnp.concatenate([cycle, interior], 1),
            precision=HIGH,
        )

    velocity = back(0, iterate, bases[0])
    velocity, bases, cycles = lax.optimization_barrier((velocity, bases[1:], cycles[1:]))
    for hop in range(1, groups):
        velocity = velocity + back(hop, cycles[hop - 1], bases[hop - 1])
    return velocity


def solution(mesh):
    placed = (
        P("fourier", None, ("ex", "ey")),
        P(("ex", "ey")),
        P("fourier", None, None),
        P("fourier", None, None),
        P("fourier", None, None),
        P(("ex", "ey")),
    )
    return jax.shard_map(
        on_device,
        mesh=mesh,
        in_specs=placed,
        out_specs=P("fourier", None, ("ex", "ey")),
        check_vma=False,
    )
```

profile of v0, /device:TPU:0, one launch (start us, length us, event | category | flops | bytes accessed | tf_op | source)
XLA Modules:
  0.0 139.8 jit_solution(10993880417799901281)
XLA Ops:
  0.0 1.2 fusion.64
  1.4 3.0 %collective-permute-start = (f32[128,16,49]{0,1,2:T(8,128)S(1)}, f32[128,16,49]{0,1,2:T(8,128)S(1)}, u32[]{:S(2)}, u32[]{:S(2)}) collective-permute-start(f32[128,16,49]{0,1,2:T(8,128)S(1)} %pad_maximum_fusion.6), channel_id=1, source_target_pairs={{0,16},{16,0},{1,17},{17,1},{2,18},{18,2},{3,19},{19,3},{4,20},{20... | collective-permute-start | bytes 1204232 | tf_op jit(solution)/shard_map/ppermute | solution.py:408
  4.6 0.9 copy.52
  5.5 0.9 copy.51
  6.5 1.2 fusion.63
  7.9 0.4 select_select_fusion
  8.3 0.4 copy-done.3
  8.6 1.4 fusion.39
  10.1 5.4 %fusion.41 = f32[64,81,128]{2,0,1:T(8,128)} fusion(f32[64,81,128]{2,0,1:T(8,128)} %param.11, f32[128,128]{1,0:T(8,128)S(1)} %select_select_fusion, s32[]{:T(128)S(6)} %select_n.133, s32[]{:T(128)S(6)} %select_n.135), kind=kOutput, calls=%fused_computation.47 | convolution fusion | flops 254803968 | bytes 5341192 | tf_op jit(solution)/shard_map/mz,zne->mne/dot_general | solution.py:414
  15.7 0.4 copy.72
  16.1 0.4 copy.73
  16.4 0.5 slice-done
  16.9 1.8 %fusion.11 = f32[64,32,128]{2,1,0:T(8,128)S(1)} fusion(f32[64,49,128]{2,0,1:T(8,128)S(1)} %slice-done, f32[64,16,49]{2,1,0:T(8,128)S(1)} %copy.73, f32[64,16,49]{2,1,0:T(8,128)S(1)} %copy.72), kind=kOutput, calls=%fused_computation.15 | convolution fusion | flops 77170688 | bytes 3055616 | tf_op jit(solution)/shard_map/mbi,mie->mbe/dot_general | solution.py:418
  18.9 1.6 %slice_subtract_fusion = f32[64,32,128]{2,0,1:T(8,128)} fusion(f32[64,81,128]{2,0,1:T(8,128)S(1)} %copy-done.1, f32[64,32,128]{2,1,0:T(8,128)S(1)} %fusion.11), kind=kLoop, calls=%fused_computation.30 | loop fusion | flops 262144 | bytes 3145728 | tf_op jit(solution)/shard_map/sub | solution.py:418
  20.5 0.6 broadcast_compare_fusion
  21.1 2.0 %copy.44 = f32[64,32,49]{2,1,0:T(8,128)} copy(f32[64,32,49]{0,1,2:T(8,128)S(1)} %copy-done.13) | data formatting | bytes 802816 | tf_op args[3]
  23.1 1.3 copy-done.7
  24.5 0.6 copy.50
  25.0 1.8 %pad_maximum_fusion.5.schur_ref = bf16[64,32,96]{2,1,0:T(8,128)(2,1)S(1)} fusion(bf16[64,32,32]{2,1,0:T(8,128)(2,1)} %get-tuple-element.32, bf16[64,32,32]{2,1,0:T(8,128)(2,1)} %get-tuple-element.31), kind=kLoop, calls=%fused_computation.36 | loop fusion | flops 1179648 | bytes 655360 | tf_op jit(solution)/shard_map/concatenate | solution.py:430
  27.1 1.2 slice-done.1
  28.3 1.9 %maximum_maximum_fusion = f32[96,49,128]{2,0,1:T(8,128)} fusion(f32[32,49,64]{2,0,1:T(8,128)S(1)} %get-tuple-element.30, f32[32,49,64]{2,0,1:T(8,128)S(1)} %get-tuple-element.29, f32[64,49,128]{2,0,1:T(8,128)S(1)} %slice-done.1), kind=kLoop, calls=%fused_computation.6 | loop fusion | flops 1204224 | bytes 4816896 | tf_op jit(solution)/shard_map/concatenate | solution.py:425
  30.4 0.6 copy-done.10
  31.0 2.0 %fusion.13 = f32[64,128,32]{1,2,0:T(8,128)S(1)} fusion(f32[64,32,49]{2,1,0:T(8,128)S(1)} %copy-done.10, f32[64,49,128]{2,0,1:T(8,128)S(1)} %slice-done.2), kind=kOutput, calls=%fused_computation.17 | convolution fusion | flops 77070336 | bytes 3055616 | tf_op jit(solution)/shard_map/mbi,mie->mbe/dot_general | solution.py:418
  32.9 12.5 %collective-permute-done.1 = f32[64,32,128]{2,0,1:T(8,128)} collective-permute-done((f32[64,32,128]{2,0,1:T(8,128)}, f32[64,32,128]{2,0,1:T(8,128)}, u32[]{:S(2)}, u32[]{:S(2)}) %collective-permute-start.1) | collective-permute-done | bytes 1048608 | tf_op jit(solution)/shard_map/ppermute | solution.py:420
  45.4 2.0 %fusion.30 = f32[64,32,128]{2,0,1:T(8,128)S(1)} fusion(f32[64,32,128]{2,0,1:T(8,128)} %collective-permute-done.1, f32[64,81,128]{2,0,1:T(8,128)S(1)} %copy-done.4, f32[64,128,32]{1,2,0:T(8,128)S(1)} %fusion.13), kind=kLoop, calls=%fused_computation.32 | loop fusion | flops 524288 | bytes 4194304 | tf_op jit(solution)/shard_map/add | solution.py:421
  47.4 0.4 collective-permute-start.2
  47.8 0.5 fusion.34
  48.3 52.9 %shard_map.109 = f32[2048,128]{1,0:T(8,128)S(1)} custom-call(f32[2048,128]{1,0:T(8,128)S(1)} %bitcast.45, bf16[64,32,96]{2,1,0:T(8,128)(2,1)S(1)} %pad_maximum_fusion.5.schur_ref, f32[1,128]{1,0:T(1,128)S(1)} %bitcast.47, f32[32,128]{1,0:T(8,128)S(1)} %get-tuple-element.19.keep_ref, f32[32,128]{1,0:T(8,128)S(1)} %get-tuple-element.20.weight_ref), custom_call_target="tpu_custom_call" | custom-call | flops 1000000000 | bytes 200000000 | tf_op jit(solution)/shard_map/pallas_call | solution.py:359
  101.2 1.6 %convolution_bitcast_fusion = f32[64,32,128]{2,0,1:T(8,128)} fusion(f32[32,64,128]{2,1,0:T(8,128)S(1)} %bitcast.46, s32[128]{0:T(128)S(1)} %copy-done.17), kind=kOutput, calls=%fused_computation.27 | convolution fusion | flops 201342976 | bytes 2097664 | tf_op jit(solution)/shard_map/bmc,ec->mbe/dot_general | solution.py:437
  102.7 2.8 %copy.58 = f32[64,32,128]{2,1,0:T(8,128)} copy(f32[64,32,128]{2,0,1:T(8,128)} %convolution_bitcast_fusion) | data formatting | bytes 2097152 | tf_op jit(solution)/shard_map/optimization_barrier | solution.py:438
  105.6 1.5 %collective-permute-start.3 = (f32[64,32,128]{2,0,1:T(8,128)}, f32[64,32,128]{2,0,1:T(8,128)}, u32[]{:S(2)}, u32[]{:S(2)}) collective-permute-start(f32[64,32,128]{2,0,1:T(8,128)} %convolution_bitcast_fusion), channel_id=1, source_target_pairs={{0,16},{16,0},{1,17},{17,1},{2,18},{18,2},{3,19},{19,3},{4,20},{20... | collective-permute-start | bytes 3145736 | tf_op jit(solution)/shard_map/ppermute | solution.py:440
  107.0 3.8 %copy.54 = f32[64,49,49]{2,1,0:T(8,128)} copy(f32[64,49,49]{0,2,1:T(8,128)} %param.15) | data formatting | bytes 1229312 | tf_op jit(solution)/shard_map/optimization_barrier | solution.py:438
  111.1 0.5 copy.74
  111.6 0.5 copy.75
  112.1 0.8 copy-done.5
  112.9 1.0 fusion.19
  113.9 0.5 copy-done.6
  114.4 2.4 %fusion.9 = f32[64,49,128]{2,1,0:T(8,128)S(1)} fusion(f32[64,49,49]{2,1,0:T(8,128)S(1)} %copy-done.6, f32[64,49,128]{2,0,1:T(8,128)S(1)} %fusion.19), kind=kOutput, calls=%fused_computation.13 | convolution fusion | flops 118013952 | bytes 3825920 | tf_op jit(solution)/shard_map/mij,mje->mie/dot_general | solution.py:457
  116.8 3.3 %bitcast_subtract_fusion = f32[64,49,128]{2,1,0:T(8,128)S(1)} fusion(f32[64,49,128]{2,1,0:T(8,128)S(1)} %fusion.9, f32[64,32,49]{2,1,0:T(8,128)S(1)} %copy-done.11, f32[128]{0:T(128)S(1)} %copy-done.25, f32[64,32,128]{2,0,1:T(8,128)} %convolution_bitcast_fusion), kind=kOutput, calls=%fused_computation.11 | convolution fusion | flops 77873152 | bytes 4661760 | tf_op jit(solution)/shard_map/mbi,mbe->mie/dot_general | solution.py:460
  120.4 1.5 %copy-done.2 = f32[64,81,128]{2,0,1:T(8,128)S(1)} copy-done((f32[64,81,128]{2,0,1:T(8,128)S(1)}, f32[64,81,128]{2,0,1:T(8,128)}, u32[]{:S(2)}) %copy-start.2) | copy-done | bytes 2654232
  121.9 0.9 fusion.22
  122.8 1.5 %fusion.2 = f32[64,81,128]{2,0,1:T(8,128)S(1)} fusion(f32[64,81,128]{2,1,0:T(8,128)S(1)} %pad_maximum_fusion, f32[128,128]{1,0:T(8,128)S(1)} %copy-done.16, s32[]{:T(128)S(6)} %select_n.133, s32[]{:T(128)S(6)} %select_n.135), kind=kOutput, calls=%fused_computation.4 | convolution fusion | flops 254803968 | bytes 5570568 | tf_op jit(solution)/shard_map/mz,mne->zne/dot_general | solution.py:461
  124.4 2.4 %fusion.25 = f32[64,49,128]{2,1,0:T(8,128)S(1)} fusion(f32[64,49,128]{2,0,1:T(8,128)S(1)} %fusion.22, f32[32,49,49]{2,1,0:T(8,128)S(1)} %copy.75, f32[32,49,49]{2,1,0:T(8,128)S(1)} %copy.74, f32[128]{0:T(128)S(1)} %copy-done.25), kind=kOutput, calls=%fused_computation.28 | convolution fusion | flops 118569024 | bytes 3826432 | tf_op jit(solution)/shard_map/mij,mje->mie/dot_general | solution.py:457
  126.8 3.8 %collective-permute-done.3 = f32[64,32,128]{2,0,1:T(8,128)} collective-permute-done((f32[64,32,128]{2,0,1:T(8,128)}, f32[64,32,128]{2,0,1:T(8,128)}, u32[]{:S(2)}, u32[]{:S(2)}) %collective-permute-start.3) | collective-permute-done | bytes 1048608 | tf_op jit(solution)/shard_map/ppermute | solution.py:440
  130.5 3.5 %fusion.31 = f32[64,49,128]{2,1,0:T(8,128)S(1)} fusion(f32[64,16,49]{2,1,0:T(8,128)S(1)} %copy-done.9, f32[64,16,49]{2,1,0:T(8,128)S(1)} %copy.72, f32[64,32,128]{2,0,1:T(8,128)} %collective-permute-done.3), kind=kOutput, calls=%fused_computation.35 | convolution fusion | flops 77170688 | bytes 3055616 | tf_op jit(solution)/shard_map/mbi,mbe->mie/dot_general | solution.py:460
  134.0 1.8 %copy.65 = f32[64,32,128]{2,1,0:T(8,128)S(1)} copy(f32[64,32,128]{2,0,1:T(8,128)} %collective-permute-done.3) | data formatting | bytes 2097152 | tf_op jit(solution)/shard_map/optimization_barrier | solution.py:469
  136.2 1.5 %fusion = f32[64,81,128]{2,0,1:T(8,128)S(1)} fusion(f32[64,81,128]{2,1,0:T(8,128)S(1)} %pad_maximum_fusion.1, f32[128,128]{1,0:T(8,128)S(1)} %copy-done.16, s32[]{:T(128)S(6)} %select_n.138, s32[]{:T(128)S(6)} %select_n.135), kind=kOutput, calls=%fused_computation.2 | convolution fusion | flops 254803968 | bytes 5570568 | tf_op jit(solution)/shard_map/mz,mne->zne/dot_general | solution.py:461
  137.7 2.0 %add.148 = f32[64,81,128]{2,0,1:T(8,128)} add(f32[64,81,128]{2,0,1:T(8,128)S(1)} %fusion.2, f32[64,81,128]{2,0,1:T(8,128)S(1)} %fusion) | non-fusion elementwise | flops 663552 | bytes 7962624 | tf_op jit(solution)/shard_map/add | solution.py:471
  (67 shorter events, 2.1 us)
Async XLA Ops:
  0.0 4.5 %copy-start.14 = (f32[64,32,32]{0,2,1:T(8,128)S(1)}, f32[64,32,32]{0,2,1:T(8,128)}, u32[]{:S(2)}) copy-start(f32[64,32,32]{0,2,1:T(8,128)} %param.13) | copy-start | bytes 786436
  1.4 14.1 %collective-permute-start = (f32[128,16,49]{0,1,2:T(8,128)S(1)}, f32[128,16,49]{0,1,2:T(8,128)S(1)}, u32[]{:S(2)}, u32[]{:S(2)}) collective-permute-start(f32[128,16,49]{0,1,2:T(8,128)S(1)} %pad_maximum_fusion.6), channel_id=1, source_target_pairs={{0,16},{16,0},{1,17},{17,1},{2,18},{18,2},{3,19},{19,3},{4,20},{20... | collective-permute-start | bytes 1204232 | tf_op jit(solution)/shard_map/ppermute | solution.py:408
  6.5 1.3 copy-start.17
  6.5 1.2 copy-start.24
  6.5 2.1 %copy-start.3 = (f32[64,81,128]{2,0,1:T(8,128)S(1)}, f32[64,81,128]{2,0,1:T(8,128)}, u32[]{:S(2)}) copy-start(f32[64,81,128]{2,0,1:T(8,128)} %param.11) | copy-start | bytes 7962628
  8.6 1.4 %copy-start.15 = (f32[128,128]{1,0:T(8,128)}, f32[128,128]{1,0:T(8,128)S(1)}, u32[]{:S(2)}) copy-start(f32[128,128]{1,0:T(8,128)S(1)} %select_select_fusion) | copy-start | bytes 196612
  10.0 5.5 %copy-start = (f32[64,81,128]{2,0,1:T(8,128)}, f32[64,81,128]{2,0,1:T(8,128)S(1)}, u32[]{:S(2)}) copy-start(f32[64,81,128]{2,0,1:T(8,128)S(1)} %fusion.39) | copy-start | bytes 7962628
  15.5 1.4 %slice-start = ((f32[64,81,128]{2,0,1:T(8,128)}), f32[64,49,128]{2,0,1:T(8,128)S(1)}, s32[]{:S(2)}) async-start(f32[64,81,128]{2,0,1:T(8,128)} %copy-done), calls=%async_computation | async-start | bytes 3211264 | tf_op jit(solution)/shard_map/slice | solution.py:418
  16.9 1.8 %copy-start.8 = (f32[64,16,49]{2,1,0:T(8,128)}, f32[64,16,49]{2,1,0:T(8,128)S(1)}, u32[]{:S(2)}) copy-start(f32[64,16,49]{2,1,0:T(8,128)S(1)} %copy.73) | copy-start | bytes 602116
  16.9 1.9 %copy-start.1 = (f32[64,81,128]{2,0,1:T(8,128)S(1)}, f32[64,81,128]{2,0,1:T(8,128)}, u32[]{:S(2)}) copy-start(f32[64,81,128]{2,0,1:T(8,128)} %copy-done) | copy-start | bytes 7962628
  18.9 2.2 %copy-start.13 = (f32[64,32,49]{0,1,2:T(8,128)S(1)}, f32[64,32,49]{0,1,2:T(8,128)}, u32[]{:S(2)}) copy-start(f32[64,32,49]{0,1,2:T(8,128)} %param.14) | copy-start | bytes 1204228
  20.5 24.9 %collective-permute-start.1 = (f32[64,32,128]{2,0,1:T(8,128)}, f32[64,32,128]{2,0,1:T(8,128)}, u32[]{:S(2)}, u32[]{:S(2)}) collective-permute-start(f32[64,32,128]{2,0,1:T(8,128)} %slice_subtract_fusion), channel_id=1, source_target_pairs={{16,0},{0,16},{17,1},{1,17},{18,2},{2,18},{19,3},{3,19},{20,4},{4,... | collective-permute-start | bytes 3145736 | tf_op jit(solution)/shard_map/ppermute | solution.py:420
  23.1 1.3 copy-start.7
  26.9 1.4 %slice-start.1 = ((f32[64,81,128]{2,0,1:T(8,128)}), f32[64,49,128]{2,0,1:T(8,128)S(1)}, s32[]{:S(2)}) async-start(f32[64,81,128]{2,0,1:T(8,128)} %param.11), calls=%async_computation.1 | async-start | bytes 3211264 | tf_op jit(solution)/shard_map/slice | solution.py:426
  28.3 1.9 %copy-start.18 = (pred[32]{0:T(512)(128)(4,1)S(1)}, pred[32]{0:T(512)(128)(4,1)}, u32[]{:S(2)}) copy-start(pred[32]{0:T(512)(128)(4,1)} %constant.173) | copy-start | bytes 100
  28.3 1.9 %copy-start.19 = (pred[32]{0:T(512)(128)(4,1)S(1)}, pred[32]{0:T(512)(128)(4,1)}, u32[]{:S(2)}) copy-start(pred[32]{0:T(512)(128)(4,1)} %constant.174) | copy-start | bytes 100
  28.3 1.9 %copy-start.20 = (pred[32]{0:T(512)(128)(4,1)S(1)}, pred[32]{0:T(512)(128)(4,1)}, u32[]{:S(2)}) copy-start(pred[32]{0:T(512)(128)(4,1)} %constant.175) | copy-start | bytes 100
  28.3 1.9 %copy-start.21 = (pred[32]{0:T(512)(128)(4,1)S(1)}, pred[32]{0:T(512)(128)(4,1)}, u32[]{:S(2)}) copy-start(pred[32]{0:T(512)(128)(4,1)} %constant.176) | copy-start | bytes 100
  28.3 1.9 %copy-start.22 = (f32[32]{0:T(128)S(1)}, f32[32]{0:T(128)}, u32[]{:S(2)}) copy-start(f32[32]{0:T(128)} %constant.177) | copy-start | bytes 388
  28.3 1.9 %copy-start.23 = (pred[128]{0:T(512)(128)(4,1)S(1)}, pred[128]{0:T(512)(128)(4,1)}, u32[]{:S(2)}) copy-start(pred[128]{0:T(512)(128)(4,1)} %get-tuple-element.44) | copy-start | bytes 388
  28.3 2.0 %slice-start.2 = ((f32[64,81,128]{2,0,1:T(8,128)}), f32[64,49,128]{2,0,1:T(8,128)S(1)}, s32[]{:S(2)}) async-start(f32[64,81,128]{2,0,1:T(8,128)} %fusion.41), calls=%async_computation.2 | async-start | bytes 3211264 | tf_op jit(solution)/shard_map/slice | solution.py:418
  28.3 2.6 %copy-start.10 = (f32[64,32,49]{2,1,0:T(8,128)S(1)}, f32[64,32,49]{2,1,0:T(8,128)}, u32[]{:S(2)}) copy-start(f32[64,32,49]{2,1,0:T(8,128)} %copy.44) | copy-start | bytes 1204228
  31.0 14.5 %copy-start.4 = (f32[64,81,128]{2,0,1:T(8,128)S(1)}, f32[64,81,128]{2,0,1:T(8,128)}, u32[]{:S(2)}) copy-start(f32[64,81,128]{2,0,1:T(8,128)} %fusion.41) | copy-start | bytes 7962628
  47.4 63.4 %collective-permute-start.2 = (f32[96,49,128]{2,0,1:T(8,128)}, f32[96,49,128]{2,0,1:T(8,128)S(1)}, u32[]{:S(2)}, u32[]{:S(2)}) collective-permute-start(f32[96,49,128]{2,0,1:T(8,128)} %maximum_maximum_fusion), channel_id=1, source_target_pairs={{0,16},{16,0},{1,17},{17,1},{2,18},{18,2},{3,19},{19,3},{4,20},{20... | collective-permute-start | bytes 7225352 | tf_op jit(solution)/shard_map/ppermute | solution.py:434
  105.6 25.0 %collective-permute-start.3 = (f32[64,32,128]{2,0,1:T(8,128)}, f32[64,32,128]{2,0,1:T(8,128)}, u32[]{:S(2)}, u32[]{:S(2)}) collective-permute-start(f32[64,32,128]{2,0,1:T(8,128)} %convolution_bitcast_fusion), channel_id=1, source_target_pairs={{0,16},{16,0},{1,17},{17,1},{2,18},{18,2},{3,19},{19,3},{4,20},{20... | collective-permute-start | bytes 3145736 | tf_op jit(solution)/shard_map/ppermute | solution.py:440
  111.1 1.8 %copy-start.5 = (f32[64,81,128]{2,0,1:T(8,128)S(1)}, f32[64,81,128]{2,0,1:T(8,128)}, u32[]{:S(2)}) copy-start(f32[64,81,128]{2,0,1:T(8,128)} %fusion.41) | copy-start | bytes 7962628
  111.1 1.7 %copy-start.16 = (f32[128,128]{1,0:T(8,128)S(1)}, f32[128,128]{1,0:T(8,128)}, u32[]{:S(2)}) copy-start(f32[128,128]{1,0:T(8,128)} %copy-done.15) | copy-start | bytes 196612
  112.9 1.5 %copy-start.6 = (f32[64,49,49]{2,1,0:T(8,128)S(1)}, f32[64,49,49]{2,1,0:T(8,128)}, u32[]{:S(2)}) copy-start(f32[64,49,49]{2,1,0:T(8,128)} %copy.54) | copy-start | bytes 1843972
  114.4 2.4 %copy-start.11 = (f32[64,32,49]{2,1,0:T(8,128)S(1)}, f32[64,32,49]{2,1,0:T(8,128)}, u32[]{:S(2)}) copy-start(f32[64,32,49]{2,1,0:T(8,128)} %copy.44) | copy-start | bytes 1204228
  114.4 2.4 %copy-start.25 = (f32[128]{0:T(128)S(1)}, f32[128]{0:T(128)}, u32[]{:S(2)}) copy-start(f32[128]{0:T(128)} %param.12) | copy-start | bytes 1540
  116.8 3.4 %copy-start.12 = (f32[64,32,128]{2,1,0:T(8,128)S(1)}, f32[64,32,128]{2,1,0:T(8,128)}, u32[]{:S(2)}) copy-start(f32[64,32,128]{2,1,0:T(8,128)} %copy.58) | copy-start | bytes 3145732
  120.2 1.8 %copy-start.2 = (f32[64,81,128]{2,0,1:T(8,128)S(1)}, f32[64,81,128]{2,0,1:T(8,128)}, u32[]{:S(2)}) copy-start(f32[64,81,128]{2,0,1:T(8,128)} %copy-done) | copy-start | bytes 7962628
  124.4 6.2 %copy-start.9 = (f32[64,16,49]{2,1,0:T(8,128)S(1)}, f32[64,16,49]{2,1,0:T(8,128)}, u32[]{:S(2)}) copy-start(f32[64,16,49]{2,1,0:T(8,128)} %copy-done.8) | copy-start | bytes 602116
where the time goes:
time: 140 us
  Pallas kernels  52.9 us (38%)
  matrix products  29.3 us (21%)
  local copies, waits for them, and re-layouts  23.4 us (17%)
  waiting for transfers between devices  16.3 us (12%)
  other arithmetic  12.4 us (9%)
  starting transfers between devices  4.94 us (4%)
    pallas_call x1, Pallas kernels, conjugate_gradients(): pl.pallas_call(functools.partial(cg_kernel, modes), out_shape=jax.ShapeDt...  52.9 us
    ppermute x1, waiting for transfers between devices, on_device(): term = lax.ppermute(term, 'fourier', [(b, a) for a, b in swap[hop]])  12.5 us
    unnamed x59, local copies, waits for them, and re-layouts  10.5 us
    dot_general x2, matrix products, back(): jnp.einsum('mbi,mbe->mie', couples[hop], cycle, precision=HIGH)  6.8 us
    dot_general x2, matrix products, on_device(): jnp.einsum('mz,zne->mne', rows_of(own_planes, order[hop]), forcing, preci...  6.79 us
    optimization_barrier x2, local copies, waits for them, and re-layouts, on_device(): iterate, inner_inv = lax.optimization_barrier((iterate, inner_inv))  6.57 us
    dot_general x2, matrix products, on_device(): jnp.einsum('mij,mje->mie', inverse, inner, precision=HIGH) / element_coef  4.8 us
    ppermute x1, waiting for transfers between devices, on_device(): lax.ppermute(iterate, 'fourier', swap[h])  3.75 us
  transfers between devices with their start and end apart: 4, of which 2 were waited for; matrix products, arithmetic and copies ran while one was open for 29% of the time, Pallas kernels for 38%

commit v1 on v0

v1 whole, which is shorter than its diff:
```python
import functools
import math
import types

import jax
import jax.numpy as jnp
from jax import lax
from jax.experimental import pallas as pl
from jax.experimental.pallas import tpu as pltpu
from jax.sharding import PartitionSpec as P

P_SIZE = 8
ITERS = 3
ELX = 8
ELY = 16
NB = 4 * P_SIZE
NI = (P_SIZE - 1) ** 2
NODES = NB + NI
DEEP = 64
TALL = 56
LANES = 128
HIGHEST = lax.Precision.HIGHEST


def dft_values(row_index, plane_index, length):
    plane_pos = plane_index.astype(jnp.float32)
    waves = ((row_index + 1) // 2).astype(jnp.float32)
    angles = 2.0 * math.pi * waves * plane_pos / length
    factor = math.sqrt(2.0 / length)
    result = jnp.where(row_index % 2 == 1, factor * jnp.cos(angles), factor * jnp.sin(angles))
    result = jnp.where(row_index == 0, 1.0 / math.sqrt(length), result)
    return jnp.where(
        row_index == length - 1, jnp.cos(math.pi * plane_pos) / math.sqrt(length), result
    )


def stacked_table(values):
    high = lax.reduce_precision(values, 8, 7)
    low = values - high
    return jnp.concatenate([high, high, low], -1).astype(jnp.bfloat16)


def split(value):
    high = value.astype(jnp.bfloat16)
    return high, (value - high.astype(jnp.float32)).astype(jnp.bfloat16)


def dot(a, b):
    return jnp.dot(a, b, preferred_element_type=jnp.float32)


def product(a, b):
    (ah, al), (bh, bl) = split(a), split(b)
    rows = a.shape[0]
    both = dot(jnp.concatenate([ah, al], 0), bh)
    return both[:rows] + (both[rows:] + dot(ah, bl))


def pile(value):
    high, low = split(value)
    return jnp.concatenate([high, low, high], 0)


def aligned(start, size):
    return pl.ds(start if isinstance(start, int) else pl.multiple_of(start, size), size)


def loop(count, unroll, body):
    while count % unroll:
        unroll -= 1

    def step(outer, carry):
        for inner in range(unroll):
            body(outer * unroll + inner)
        return carry

    lax.fori_loop(0, count // unroll, step, 0)


class Plan:
    def __init__(self, sizes, modes, planes):
        self.groups, self.ex, self.ey = sizes
        self.modes, self.planes = modes, planes
        self.all_modes = self.groups * modes
        self.chunk = min(16, modes)
        self.chunks = modes // self.chunk
        self.fold = max(1, LANES // modes)
        self.couple_rows = NB // self.fold
        self.couple_ways = 2 if self.ey % 2 == 0 else 1
        step = 8 * self.couple_ways
        self.couple_part = -(-NI * self.couple_rows // step) * 8
        self.couple_all = max(DEEP * self.couple_rows, self.couple_part * self.couple_ways)
        self.inner_rows = -(-NI // self.fold)
        self.inner_ways = self.ey
        self.inner_part = -(-self.inner_rows * TALL // (8 * self.inner_ways)) * 8
        self.inner_all = self.inner_part * self.inner_ways
        self.peers = self.ex * self.ey - 1


def layout(p):
    f32 = lambda *dims: pltpu.VMEM(dims, jnp.float32)
    half = lambda *dims: pltpu.VMEM(dims, jnp.bfloat16)
    dma = lambda *dims: pltpu.SemaphoreType.DMA(dims)
    far, m, z = p.groups - 1, p.modes, p.planes
    field = f32(NB * m, LANES)
    rows = NB * p.chunk
    return dict(
        f=f32(NODES, z, LANES),
        fo=f32(far, NI, z, LANES),
        spec=f32((NB + DEEP) * p.all_modes, LANES),
        res=field,
        app=field,
        x=field,
        dir=field,
        along=field,
        cin=f32(NI, NB, m),
        sin=f32(NB, NB, m),
        iin=f32(NI, NI, m),
        cpack=f32(p.groups, p.couple_all, LANES),
        ipack=f32(p.groups, p.inner_all, LANES),
        cf=f32(p.all_modes * NB, LANES),
        ct=f32(p.all_modes * DEEP, LANES),
        invf=f32(p.all_modes * TALL, LANES),
        sch=f32(m * NB, LANES),
        cbuf=f32(rows, LANES),
        sbuf=f32(far, p.chunks, rows, LANES),
        rbuf=f32(far, p.chunks, rows, LANES),
        xe=f32(p.chunks, rows, LANES),
        xr=f32(far, p.chunks, rows, LANES),
        one=half(LANES, LANES),
        oneT=half(LANES, LANES),
        scale=f32(8, LANES),
        keep=f32(NB, LANES),
        weight=f32(NB, LANES),
        xs=f32(ITERS, 2, 2, m, LANES),
        xh=f32(ITERS, 2, 2, m, LANES),
        ys=f32(ITERS, 2, m, LANES),
        yh=f32(ITERS, 3, 2, m, LANES),
        ps=f32(ITERS, 1, 2 * m),
        pr=f32(ITERS, p.peers, 1, 2 * m),
        s_local=dma(5),
        s_halo=dma(2, ITERS, 8),
        s_sum=dma(2, ITERS, p.peers),
        s_cx=dma(2, far),
        s_cy=dma(2, far, max(1, p.couple_ways - 1)),
        s_ix=dma(2, far),
        s_iy=dma(2, far, max(1, p.inner_ways - 1)),
        s_f1=dma(2, far, p.chunks),
        s_f2=dma(2, far),
        s_b1=dma(2, far, p.chunks),
    )


def kernel(p, names, forcing, coef_ref, cell_ref, schur_in, couple_in, inner_in, fwd, back_own, back_far, out, *refs):
    s = types.SimpleNamespace(**dict(zip(names, refs)))
    m, z, gm, mc = p.modes, p.planes, p.all_modes, p.chunk
    cells = LANES
    sizes = {"fourier": p.groups, "ex": p.ex, "ey": p.ey}
    place = {axis: lax.axis_index(axis) for axis in sizes}
    lane = lax.broadcasted_iota(jnp.int32, (m, cells), 1)
    lane_row = lane // ELY
    lane_col = lane % ELY

    def shifted(axis, by):
        return lax.rem(place[axis] + (by % sizes[axis]), sizes[axis])

    def remote(source, target, sems, index, device):
        return pltpu.make_async_remote_copy(
            src_ref=source,
            dst_ref=target,
            send_sem=sems.at[(0,) + index],
            recv_sem=sems.at[(1,) + index],
            device_id=device,
            device_id_type=pl.DeviceIdType.MESH,
        )

    hops = range(1, p.groups)
    around = [(a, b) for a in range(p.ex) for b in range(p.ey) if a or b]

    loads = [
        pltpu.make_async_copy(couple_in, s.cin, s.s_local.at[0]),
        pltpu.make_async_copy(inner_in, s.iin, s.s_local.at[1]),
        pltpu.make_async_copy(
            forcing.at[pl.ds(NB, NI)], s.f.at[pl.ds(NB, NI)], s.s_local.at[2]
        ),
        pltpu.make_async_copy(forcing.at[pl.ds(0, NB)], s.f.at[pl.ds(0, NB)], s.s_local.at[3]),
        pltpu.make_async_copy(schur_in, s.sin, s.s_local.at[4]),
    ]
    for load in loads:
        load.start()

    s.xh[...] = jnp.zeros_like(s.xh)
    s.yh[...] = jnp.zeros_like(s.yh)

    barrier = pltpu.get_barrier_semaphore()
    for a, b in around:
        pl.semaphore_signal(
            barrier,
            inc=1,
            device_id={"ex": shifted("ex", a), "ey": shifted("ey", b)},
            device_id_type=pl.DeviceIdType.MESH,
        )
    for hop in hops:
        pl.semaphore_signal(
            barrier,
            inc=1,
            device_id={"fourier": shifted("fourier", hop)},
            device_id_type=pl.DeviceIdType.MESH,
        )

    def clear(ref, start, stop):
        if stop > start:
            ref[pl.ds(start, stop - start), :] = jnp.zeros((stop - start, LANES), jnp.float32)

    br = p.couple_rows
    own_rows = NI * br
    got_rows = p.couple_part * p.couple_ways
    clear(s.cpack.at[0], own_rows, p.couple_all)
    for g in hops:
        clear(s.cpack.at[g], got_rows, p.couple_all)
    loads[0].wait()
    for i in range(NI):
        s.cpack[0, i * br : (i + 1) * br, :] = jnp.concatenate(
            [s.cin[i, k * br : (k + 1) * br, :] for k in range(p.fold)], 1
        )
    pl.semaphore_wait(barrier, len(around) + p.groups - 1)

    def share_out(pack, part, ways, sem_x, sem_y):
        turn = lax.rem(place["ey"], ways)
        rows = aligned(turn * part, part) if part % 8 else pl.ds(pl.multiple_of(turn * part, 8), part)
        across = [
            remote(
                pack.at[0, rows], pack.at[g, rows], sem_x, (g - 1,),
                {"fourier": shifted("fourier", g)},
            )
            for g in hops
        ]
        beside = [
            remote(
                pack.at[g, rows], pack.at[g, rows], sem_y, (g - 1, k - 1),
                {"ey": place["ey"] - turn + lax.rem(turn + k, ways)},
            )
            for g in hops
            for k in range(1, ways)
        ]
        return across, beside

    couple_x, couple_y = share_out(s.cpack, p.couple_part, p.couple_ways, s.s_cx, s.s_cy)
    inner_x, inner_y = share_out(s.ipack, p.inner_part, p.inner_ways, s.s_ix, s.s_iy)
    for copy in couple_x:
        copy.start()

    loads[1].wait()
    ir = p.inner_rows
    clear(s.ipack.at[0], 0, p.inner_all)
    for i in range(ir):
        picks = [s.iin[min(k * ir + i, NI - 1), :, :] for k in range(p.fold)]
        s.ipack[0, i * TALL : i * TALL + NI, :] = jnp.concatenate(picks, 1)
    for copy in inner_x:
        copy.start()

    lines = lax.broadcasted_iota(jnp.int32, (LANES, LANES), 0)
    hot = jnp.where(lines == cell_ref[0:1, :], 1.0, 0.0).astype(jnp.float32)
    hot_t = jnp.transpose(hot)
    s.oneT[...] = hot.astype(jnp.bfloat16)
    s.one[...] = hot_t.astype(jnp.bfloat16)
    s.scale[...] = lax.dot_general(
        jnp.broadcast_to(coef_ref[0:1, :], (8, LANES)),
        hot_t,
        (((1,), (0,)), ((), ())),
        precision=HIGHEST,
        preferred_element_type=jnp.float32,
    )

    def flat(pack, g, start, count, stride, width):
        rows = pack[g, pl.ds(start, count, stride=stride) if stride > 1 else pl.ds(start, count), :]
        if count < LANES:
            rows = jnp.concatenate([rows, jnp.zeros((LANES - count, LANES), jnp.float32)], 0)
        return jnp.transpose(rows)

    def couple_matrices(g):
        for b in range(br):
            turned_rows = flat(s.cpack, g, b, DEEP, br, NI)
            for k in range(p.fold):
                s.cf[pl.ds(g * m * NB + k * br + b, m, stride=NB), :] = turned_rows[
                    k * m : (k + 1) * m
                ]

    def inner_matrices(g):
        for i in range(ir):
            turned_rows = flat(s.ipack, g, i * TALL, TALL, 1, NI)
            for k in range(p.fold):
                if k * ir + i < TALL:
                    s.invf[pl.ds(g * m * TALL + k * ir + i, m, stride=TALL), :] = turned_rows[
                        k * m : (k + 1) * m
                    ]

    def spectrum(n):
        s.spec[aligned(n * gm, gm), :] = dot(fwd[0], pile(s.f[n]))

    clear(s.spec, NODES * gm, (NB + DEEP) * gm)
    loads[2].wait()
    loop(NI, 7, lambda n: spectrum(NB + n))
    loads[3].wait()
    loop(NB, 8, spectrum)
    couple_matrices(0)

    def permuted(rows, hot_ref):
        high, low = split(rows)
        both = dot(jnp.concatenate([high, low], 0), hot_ref[...])
        return both[: rows.shape[0]] + both[rows.shape[0] :]

    def condense(g, c, store):
        def one_mode(k):
            j = g * m + c * mc + k
            inner = s.spec[pl.ds(NB * gm + j, DEEP, stride=gm), :]
            matrix = s.cf[aligned(j * NB, NB), :DEEP]
            s.cbuf[pl.ds(k, NB, stride=mc), :] = s.spec[
                pl.ds(j, NB, stride=gm), :
            ] - product(matrix, inner)

        loop(mc, 8, one_mode)
        for block in range(NB * mc // LANES):
            store(block, permuted(s.cbuf[block * LANES : (block + 1) * LANES, :], s.one))

    def keep_own(c):
        per = LANES // mc

        def store(block, rows):
            for k in range(per):
                n = block * per + k
                s.res[n * m + c * mc : n * m + (c + 1) * mc, :] = rows[k * mc : (k + 1) * mc]

        return store

    for copy in couple_x:
        copy.wait_recv()
    for copy in couple_y:
        copy.start()
    condense(0, 0, keep_own(0))
    for copy in couple_y:
        copy.wait_recv()

    first = []
    for g in hops:
        couple_matrices(g)
        for c in range(p.chunks):

            def store(block, rows, g=g, c=c):
                s.sbuf[g - 1, c, block * LANES : (block + 1) * LANES, :] = rows

            condense(g, c, store)
            copy = remote(
                s.sbuf.at[g - 1, c], s.rbuf.at[g - 1, c], s.s_f1, (g - 1, c),
                {"fourier": shifted("fourier", -g)},
            )
            copy.start()
            first.append((g, c, copy))

    second = []
    for g in hops:
        copy = remote(
            forcing.at[pl.ds(NB, NI)], s.fo.at[g - 1], s.s_f2, (g - 1,),
            {"fourier": shifted("fourier", g)},
        )
        copy.start()
        second.append(copy)
    for copy in inner_x:
        copy.wait_recv()
    for copy in inner_y:
        copy.start()

    for c in range(1, p.chunks):
        condense(0, c, keep_own(c))

    loads[4].wait()
    for a in range(NB):
        rows = s.sin[a]
        high = rows.astype(jnp.bfloat16).astype(jnp.float32)
        rows = jnp.concatenate([high, high, rows - high, jnp.zeros_like(rows)], 0)
        if m < LANES:
            rows = jnp.concatenate([rows, jnp.zeros((LANES, LANES - m), jnp.float32)], 1)
        s.sch[pl.ds(a, m, stride=NB), :] = jnp.transpose(rows)[:m]

    slots = lax.broadcasted_iota(jnp.int32, (NB, cells), 0)
    places = lax.broadcasted_iota(jnp.int32, (NB, cells), 1)
    row_ids = place["ex"] * ELX + places // ELY
    col_ids = place["ey"] * ELY + places % ELY
    dropped = (
        ((slots == 0) | (slots >= 3 * P_SIZE)) & (row_ids == 0)
        | (slots >= P_SIZE) & (slots <= 2 * P_SIZE) & (row_ids == ELX * p.ex - 1)
        | (slots <= P_SIZE) & (col_ids == 0)
        | (slots >= 2 * P_SIZE) & (slots <= 3 * P_SIZE) & (col_ids == ELY * p.ey - 1)
    )
    keep = jnp.where(dropped, 0.0, 1.0).astype(jnp.float32)
    s.keep[...] = keep
    s.weight[...] = keep * jnp.where(slots % P_SIZE == 0, 0.25, 0.5)
    for ref in (s.x, s.dir, s.along):
        ref[...] = jnp.zeros_like(ref)

    def couple_turned(q):
        square = jnp.transpose(s.cf[aligned(q * LANES, LANES), :])
        for k in range(LANES // NB):
            piece = square[:DEEP] if k == 0 else pltpu.roll(square[:DEEP], LANES - k * NB, 1)
            s.ct[aligned((q * (LANES // NB) + k) * DEEP, DEEP), :] = piece

    loop(gm * NB // LANES, 4, couple_turned)
    inner_matrices(0)
    for copy in inner_y:
        copy.wait_recv()
    for g in hops:
        inner_matrices(g)

    def node(n):
        return aligned(n * m, m)

    def turned(value, shift):
        shift = shift % cells
        return pltpu.roll(value, shift, 1) if shift else value

    def exists(axis, step):
        if step == 0:
            return None
        return place[axis] < sizes[axis] - 1 if step > 0 else place[axis] > 0

    def guarded(ex_step, ey_step, action):
        tests = [t for t in (exists("ex", ex_step), exists("ey", ey_step)) if t is not None]
        pl.when(functools.reduce(jnp.logical_and, tests))(action)

    def halo_copy(turn, number, source, target, ex_step, ey_step):
        copy = pltpu.make_async_remote_copy(
            src_ref=source,
            dst_ref=target,
            send_sem=s.s_halo.at[0, turn, number],
            recv_sem=s.s_halo.at[1, turn, number],
            device_id={"ex": shifted("ex", ex_step), "ey": shifted("ey", ey_step)},
            device_id_type=pl.DeviceIdType.MESH,
        )
        guarded(ex_step, ey_step, copy.start)
        return (
            lambda: guarded(-ex_step, -ey_step, copy.wait_recv),
            lambda: guarded(ex_step, ey_step, copy.wait_send),
        )

    def assemble(ref, turn):
        bottom = lambda k: k
        top = lambda k: 3 * P_SIZE - k
        left = lambda k: (NB - k) % NB
        right = lambda k: P_SIZE + k
        last = cells - ELY
        copies = []
        up = jnp.zeros((m, cells), jnp.float32)
        down = up
        for k in range(P_SIZE + 1):
            up = jnp.where(lane_col == k, turned(ref[node(top(k)), :], k - ELY + 1), up)
            down = jnp.where(lane_col == k, turned(ref[node(bottom(k)), :], k), down)
        s.ys[turn, 0] = up
        s.ys[turn, 1] = down
        for slot, ex_step in ((1, 1), (2, -1), (0, 0)):
            for way, ey_step in ((0, 1), (1, -1)):
                copies.append(
                    halo_copy(
                        turn, 2 * slot + way, s.ys.at[turn, way], s.yh.at[turn, slot, way],
                        ex_step, ey_step,
                    )
                )
        up = jnp.zeros((m, cells), jnp.float32)
        down = up
        for k in range(P_SIZE):
            up = jnp.where(lane_row == k, turned(ref[node(right(k)), :], ELY * k - last), up)
            down = jnp.where(lane_row == k, turned(ref[node(left(k)), :], ELY * k), down)
        s.xs[turn, 0, 0] = up
        s.xs[turn, 1, 0] = down
        s.xs[turn, 0, 1] = turned(ref[node(right(P_SIZE)), :], -last)
        s.xs[turn, 1, 1] = ref[node(left(P_SIZE)), :]
        for way, ex_step in ((0, 1), (1, -1)):
            copies.append(
                halo_copy(turn, 6 + way, s.xs.at[turn, way], s.xh.at[turn, way], ex_step, 0)
            )

        for k in range(P_SIZE + 1):
            here_left, here_right = ref[node(left(k)), :], ref[node(right(k)), :]
            ref[node(left(k)), :] = here_left + jnp.where(
                lane_row == 0, 0.0, turned(here_right, ELY)
            )
            ref[node(right(k)), :] = here_right + jnp.where(
                lane_row == ELX - 1, 0.0, turned(here_left, -ELY)
            )
        for arrive, _ in copies:
            arrive()

        for k in range(P_SIZE + 1):
            part, lanes = divmod(k, P_SIZE)
            low = turned(s.xh[turn, 0, part], -ELY * lanes)
            high = turned(s.xh[turn, 1, part], last - ELY * lanes)
            for n, halo, row in ((left(k), low, 0), (right(k), high, ELX - 1)):
                value = ref[node(n), :] + jnp.where(lane_row == row, halo, 0.0)
                if n % (2 * P_SIZE) > P_SIZE:
                    value = value * s.keep[n : n + 1, :]
                ref[node(n), :] = value

        lines = []
        for way in range(2):
            line = s.yh[turn, 0, way]
            before = jnp.where(
                lane == 0, turned(s.yh[turn, 1, way], P_SIZE), turned(line, P_SIZE)
            )
            after = jnp.where(
                lane == last + P_SIZE, turned(s.yh[turn, 2, way], -P_SIZE), turned(line, -P_SIZE)
            )
            lines.append(
                line
                + jnp.where(lane_col == 0, before, jnp.where(lane_col == P_SIZE, after, 0.0))
            )
        low_all, high_all = lines
        for k in range(P_SIZE + 1):
            b, t = bottom(k), top(k)
            here_bottom, here_top = ref[node(b), :], ref[node(t), :]
            ref[node(b), :] = s.keep[b : b + 1, :] * (
                here_bottom
                + jnp.where(lane_col == 0, turned(low_all, -k), turned(here_top, 1))
            )
            ref[node(t), :] = s.keep[t : t + 1, :] * (
                here_top
                + jnp.where(
                    lane_col == ELY - 1, turned(high_all, ELY - 1 - k), turned(here_bottom, -1)
                )
            )
        for _, leave in copies:
            leave()

    def operator():
        scale = s.scale[0:1, :]

        def one_mode(k):
            value = s.res[pl.ds(k, NB, stride=m), :]
            matrix = s.sch[aligned(k * NB, NB), : 3 * NB].astype(jnp.bfloat16)
            s.app[pl.ds(k, NB, stride=m), :] = dot(matrix, pile(value)) * scale

        loop(m, 8, one_mode)

    def sums_start(turn):
        def step(outer, sums):
            norm, curve = sums
            for inner in range(4):
                n = outer * 4 + inner
                mine = s.res[node(n), :]
                norm = norm + s.weight[pl.ds(n, 1), :] * mine * mine
                curve = curve + mine * s.app[node(n), :]
            return norm, curve

        zero = jnp.zeros((m, cells), jnp.float32)
        norm, curve = lax.fori_loop(0, NB // 4, step, (zero, zero))
        total = lax.dot_general(
            jnp.ones((8, cells), jnp.float32),
            jnp.concatenate([norm, curve], 0),
            (((1,), (1,)), ((), ())),
            precision=HIGHEST,
            preferred_element_type=jnp.float32,
        )
        s.ps[turn] = total[0:1, :]
        copies = [
            remote(
                s.ps.at[turn], s.pr.at[turn, k], s.s_sum, (turn, k),
                {"ex": shifted("ex", a), "ey": shifted("ey", b)},
            )
            for k, (a, b) in enumerate(around)
        ]
        for copy in copies:
            copy.start()
        return copies

    def sums_end(turn, copies):
        total = s.ps[turn]
        for k, copy in enumerate(copies):
            copy.wait_recv()
            total = total + s.pr[turn, k]
        for copy in copies:
            copy.wait_send()
        row = lax.broadcasted_iota(jnp.int32, (m, 2 * m), 0)
        column = lax.broadcasted_iota(jnp.int32, (m, 2 * m), 1)
        pick = lambda offset: jnp.sum(
            jnp.where(column == row + offset, total, 0.0), axis=1, keepdims=True
        )
        return pick(0), pick(m)

    for g, c, copy in first:
        copy.wait_recv()

        def add(n, g=g, c=c):
            rows = aligned(n * m + c * mc, mc)
            s.res[rows, :] = s.res[rows, :] + s.rbuf[g - 1, c, aligned(n * mc, mc), :]

        loop(NB, 8, add)
    assemble(s.res, 0)

    def scalars(turn, norm, curve, norm_before, step_before):
        ratio = jnp.where(turn == 0, 0.0, norm / norm_before)
        return ratio, norm / (curve - ratio * norm / step_before)

    def sweep(turn, carry):
        operator()
        copies = sums_start(turn)
        assemble(s.app, turn + 1)
        norm, curve = sums_end(turn, copies)
        ratio, step_size = scalars(turn, norm, curve, *carry)

        def update(n):
            rows = node(n)
            search = s.res[rows, :] + ratio * s.dir[rows, :]
            along = s.app[rows, :] + ratio * s.along[rows, :]
            s.x[rows, :] = s.x[rows, :] + step_size * search
            s.dir[rows, :] = search
            s.along[rows, :] = along
            s.res[rows, :] = s.res[rows, :] - step_size * along

        loop(NB, 4, update)
        return norm, step_size

    one = jnp.ones((m, 1), jnp.float32)
    carry = lax.fori_loop(0, ITERS - 1, sweep, (one, one))
    operator()
    norm, curve = sums_end(ITERS - 1, sums_start(ITERS - 1))
    ratio, step_size = scalars(ITERS - 1, norm, curve, *carry)

    def finish(n):
        rows = node(n)
        s.x[rows, :] = s.x[rows, :] + step_size * (s.res[rows, :] + ratio * s.dir[rows, :])

    loop(NB, 4, finish)

    per = LANES // mc
    third = []
    for c in range(p.chunks):
        for block in range(NB // per):
            rows = jnp.concatenate(
                [
                    s.x[n * m + c * mc : n * m + (c + 1) * mc, :]
                    for n in range(block * per, (block + 1) * per)
                ],
                0,
            )
            s.xe[c, block * LANES : (block + 1) * LANES, :] = permuted(rows, s.oneT)
        for g in hops:
            copy = remote(
                s.xe.at[c], s.xr.at[g - 1, c], s.s_b1, (g - 1, c),
                {"fourier": shifted("fourier", g)},
            )
            copy.start()
            third.append((g, c, copy))

    for copy in second:
        copy.wait_recv()

    def add_far(n):
        rows = aligned((NB + n) * gm, gm)
        total = s.spec[rows, :]
        for g in hops:
            total = total + dot(fwd[g], pile(s.fo[g - 1, n]))
        s.spec[rows, :] = total

    loop(NI, 7, add_far)
    inverse_coef = 1.0 / coef_ref[0:1, :]

    def base(j):
        inner = s.spec[pl.ds(NB * gm + j, DEEP, stride=gm), :]
        matrix = s.invf[pl.ds(pl.multiple_of(j * TALL, 8), TALL), :DEEP]
        value = product(matrix, inner) * inverse_coef
        s.spec[pl.ds(NB * gm + j, NI, stride=gm), :] = value[:NI]

    loop(gm, 4, base)

    def place_cycle(g, c, source):
        def interior(k):
            j = g * m + c * mc + k
            matrix = s.ct[aligned(j * DEEP, DEEP), :NB]
            value = product(matrix, source[pl.ds(k, NB, stride=mc), :])
            rows = pl.ds(NB * gm + j, NI, stride=gm)
            s.spec[rows, :] = s.spec[rows, :] - value[:NI]

        loop(mc, 4, interior)

        def cycle(n):
            s.spec[aligned(n * gm + g * m + c * mc, mc), :] = source[aligned(n * mc, mc), :]

        loop(NB, 8, cycle)

    for c in range(p.chunks):
        place_cycle(0, c, s.xe.at[c])

    def own_velocity(n):
        out[n] = dot(back_own[...], pile(s.spec[aligned(n * gm, m), :]))

    loop(NODES, 9, own_velocity)

    for g, c, copy in third:
        copy.wait_recv()
        place_cycle(g, c, s.xr.at[g - 1, c])

        def far_velocity(n, g=g, c=c):
            rows = s.spec[aligned(n * gm + g * m + c * mc, mc), :]
            out[n] = out[n] + dot(back_far[(g - 1) * p.chunks + c], pile(rows))

        loop(NODES, 9, far_velocity)

    for copy in couple_x + couple_y + inner_x + inner_y + second:
        copy.wait_send()
    for _, _, copy in first + third:
        copy.wait_send()


def on_device(forcing, element_coef, schur, couple, inner_inv, element_cell):
    planes, _, elements = forcing.shape
    modes = schur.shape[0]
    sizes = tuple(lax.axis_size(axis) for axis in ("fourier", "ex", "ey"))
    p = Plan(sizes, modes, planes)
    me = lax.axis_index("fourier")
    length = planes * p.groups

    def group_of(hop):
        return lax.rem(me + p.groups - hop, p.groups)

    def iota(shape, dim):
        return lax.broadcasted_iota(jnp.int32, shape, dim)

    dims = (p.groups, p.all_modes, planes)
    mode = group_of(iota(dims, 1) // modes) * modes + iota(dims, 1) % modes
    plane = group_of(iota(dims, 0)) * planes + iota(dims, 2)
    fwd = stacked_table(dft_values(mode, plane, length))
    dims = (planes, modes)
    back_own = stacked_table(
        dft_values(me * modes + iota(dims, 1), me * planes + iota(dims, 0), length)
    )
    dims = ((p.groups - 1) * p.chunks, planes, p.chunk)
    hop = 1 + iota(dims, 0) // p.chunks
    mode = group_of(hop) * modes + iota(dims, 0) % p.chunks * p.chunk + iota(dims, 2)
    back_far = stacked_table(dft_values(mode, me * planes + iota(dims, 1), length))

    scratch = layout(p)
    whole = pl.BlockSpec(memory_space=pltpu.VMEM)
    stay = pl.BlockSpec(memory_space=pl.ANY)
    velocity = pl.pallas_call(
        functools.partial(kernel, p, tuple(scratch)),
        out_shape=jax.ShapeDtypeStruct((NODES, planes, elements), jnp.float32),
        in_specs=[stay, whole, whole, stay, stay, stay, whole, whole, whole],
        out_specs=whole,
        scratch_shapes=list(scratch.values()),
        compiler_params=pltpu.CompilerParams(
            collective_id=0, has_side_effects=True, vmem_limit_bytes=60 << 20
        ),
        cost_estimate=pl.CostEstimate(flops=10**9, bytes_accessed=2 * 10**8, transcendentals=0),
    )(
        jnp.transpose(forcing, (1, 0, 2)),
        element_coef[None],
        element_cell[None],
        jnp.transpose(schur, (1, 2, 0)),
        jnp.transpose(couple, (2, 1, 0)),
        jnp.transpose(inner_inv, (1, 2, 0)),
        fwd,
        back_own,
        back_far,
    )
    return jnp.transpose(velocity, (1, 0, 2))


def solution(mesh):
    placed = (
        P("fourier", None, ("ex", "ey")),
        P(("ex", "ey")),
        P("fourier", None, None),
        P("fourier", None, None),
        P("fourier", None, None),
        P(("ex", "ey")),
    )
    return jax.shard_map(
        on_device,
        mesh=mesh,
        in_specs=placed,
        out_specs=P("fourier", None, ("ex", "ey")),
        check_vma=False,
    )
```

time: 140 us -> 116 us (0.83)
  Pallas kernels: 52.9 us -> 109 us
  matrix products: 29.3 us -> 0 us
  local copies, waits for them, and re-layouts: 23.4 us -> 3.59 us
  waiting for transfers between devices: 16.3 us -> 0 us
  other arithmetic: 12.4 us -> 3.93 us
  starting transfers between devices: 4.94 us -> 0 us
    pallas_call x1, Pallas kernels: 52.9 us -> 109 us  [on_device(): pl.pallas_call(functools.partial(kernel, p, tuple(scratch)), out_shape=ja...]
    dot_general x15 -> x0, matrix products: 29.3 us -> none  [the longest x2 6.8 us: back(): jnp.einsum('mbi,mbe->mie', couples[hop], cycle, precision=HIGH)]
    ppermute x4 -> x0, waiting for transfers between devices: 16.3 us -> none  [the longest x1 12.5 us: on_device(): term = lax.ppermute(term, 'fourier', [(b, a) for a, b in swap[hop]])]
    optimization_barrier x3 -> x0, local copies, waits for them, and re-layouts: 8.4 us -> none  [the longest x2 6.57 us: on_device(): iterate, inner_inv = lax.optimization_barrier((iterate, inner_inv))]
    unnamed x59 -> x1, local copies, waits for them, and re-layouts: 10.5 us -> 3.59 us
    ppermute x4 -> x0, starting transfers between devices: 4.94 us -> none  [the longest x1 3.03 us: on_device(): arrived = lax.ppermute(folded, 'fourier', swap[hop])]
    add x2, other arithmetic: 3.99 us -> 0.01 us  [the longest x1 0.01 us: on_device(): mode = group_of(iota(dims, 1) // modes) * modes + iota(dims, 1) % modes]
    slice x10 -> x0, local copies, waits for them, and re-layouts: 3.61 us -> none  [the longest x2 1.24 us: on_device(): forcing[:, NB:]]
  transfers between devices with their start and end apart: 4 -> 0, of which waited for: 2 -> 0; matrix products, arithmetic and copies ran while one was open for 29% -> 0% of each run, Pallas kernels for 38% -> 0%
where the time goes in v1:
time: 116 us
  Pallas kernels  109 us (94%)
  other arithmetic  3.93 us (3%)
  local copies, waits for them, and re-layouts  3.59 us (3%)
    pallas_call x1, Pallas kernels, on_device(): pl.pallas_call(functools.partial(kernel, p, tuple(scratch)), out_shape=ja...  109 us
    unnamed x1, local copies, waits for them, and re-layouts  3.59 us

profile of v1, /device:TPU:0, one launch (start us, length us, event | category | flops | bytes accessed | tf_op | source)
XLA Modules:
  0.0 116.2 jit_solution(17545922627625308560)
XLA Ops:
  0.2 0.2 reduce-precision_convert_fusion.2
  0.4 0.7 pad_maximum_fusion.2.back_own
  1.1 0.8 reduce-precision_convert_fusion.1
  1.9 0.8 pad_maximum_fusion.fwd
  2.6 0.6 reduce-precision_convert_fusion
  3.3 0.7 pad_maximum_fusion.1.back_far
  4.0 108.6 %shard_map.64 = f32[81,64,128]{2,1,0:T(8,128)} custom-call(f32[81,64,128]{2,1,0:T(8,128)} %bitcast.8, f32[1,128]{1,0:T(1,128)} %bitcast.12, s32[1,128]{1,0:T(1,128)} %bitcast.13, f32[32,32,64]{2,1,0:T(8,128)} %bitcast.11, f32[49,32,64]{2,1,0:T(8,128)} %bitcast.10, f32[49,49,64]{2,1,0:T(8,128)} %bitcast.9, bf16[2,128,192]{2,1,0:T(8,128)(2,1)} %pad_maximum_fusion.fwd, ...), custom_call_target="tpu_custom_call" | custom-call | flops 1000000000 | bytes 200000000 | tf_op jit(solution)/shard_map/pallas_call | solution.py:742
  112.6 3.6 %copy.8 = f32[64,81,128]{2,0,1:T(8,128)} copy(f32[64,81,128]{2,0,1:T(8,128)} %bitcast.7) | data formatting | bytes 5308416
  (13 shorter events, 0.1 us)

commit v2 on v1

--- a/solution.py
+++ b/solution.py
@@ -19,6 +19,7 @@
 DEEP = 64
 TALL = 56
 LANES = 128
+PLANES = 2 * P_SIZE + 1
 HIGHEST = lax.Precision.HIGHEST
 
 
@@ -34,10 +35,9 @@
     )
 
 
-def stacked_table(values):
-    high = lax.reduce_precision(values, 8, 7)
-    low = values - high
-    return jnp.concatenate([high, high, low], -1).astype(jnp.bfloat16)
+def stacked(values):
+    high = values.astype(jnp.bfloat16).astype(jnp.float32)
+    return jnp.concatenate([high, high, values - high], 1).astype(jnp.bfloat16)
 
 
 def split(value):
@@ -63,6 +63,10 @@
 
 def aligned(start, size):
     return pl.ds(start if isinstance(start, int) else pl.multiple_of(start, size), size)
+
+
+def tile(start, size):
+    return pl.ds(start if isinstance(start, int) else pl.multiple_of(start, 8), size)
 
 
 def loop(count, unroll, body):
@@ -84,17 +88,24 @@
         self.all_modes = self.groups * modes
         self.chunk = min(16, modes)
         self.chunks = modes // self.chunk
+        self.part = min(32, modes)
+        self.parts = modes // self.part
+        self.part_pitch = self.part + 8
         self.fold = max(1, LANES // modes)
         self.couple_rows = NB // self.fold
-        self.couple_ways = 2 if self.ey % 2 == 0 else 1
+        self.couple_ways = self.ey
         step = 8 * self.couple_ways
         self.couple_part = -(-NI * self.couple_rows // step) * 8
         self.couple_all = max(DEEP * self.couple_rows, self.couple_part * self.couple_ways)
         self.inner_rows = -(-NI // self.fold)
-        self.inner_ways = self.ey
+        self.inner_ways = self.ex * self.ey
         self.inner_part = -(-self.inner_rows * TALL // (8 * self.inner_ways)) * 8
         self.inner_all = self.inner_part * self.inner_ways
         self.peers = self.ex * self.ey - 1
+        self.pitch = modes + 8
+        self.all_pitch = self.all_modes + 8
+        self.chunk_pitch = self.chunk + 8
+        self.matrix = NB + 8
 
 
 def layout(p):
@@ -102,12 +113,11 @@
     half = lambda *dims: pltpu.VMEM(dims, jnp.bfloat16)
     dma = lambda *dims: pltpu.SemaphoreType.DMA(dims)
     far, m, z = p.groups - 1, p.modes, p.planes
-    field = f32(NB * m, LANES)
-    rows = NB * p.chunk
+    field = f32(NB * p.pitch, LANES)
     return dict(
         f=f32(NODES, z, LANES),
         fo=f32(far, NI, z, LANES),
-        spec=f32((NB + DEEP) * p.all_modes, LANES),
+        spec=f32((NB + DEEP) * p.all_pitch, LANES),
         res=field,
         app=field,
         x=field,
@@ -118,18 +128,25 @@
         iin=f32(NI, NI, m),
         cpack=f32(p.groups, p.couple_all, LANES),
         ipack=f32(p.groups, p.inner_all, LANES),
-        cf=f32(p.all_modes * NB, LANES),
+        cf=f32(p.all_modes * p.matrix, LANES),
         ct=f32(p.all_modes * DEEP, LANES),
         invf=f32(p.all_modes * TALL, LANES),
-        sch=f32(m * NB, LANES),
-        cbuf=f32(rows, LANES),
-        sbuf=f32(far, p.chunks, rows, LANES),
-        rbuf=f32(far, p.chunks, rows, LANES),
-        xe=f32(p.chunks, rows, LANES),
-        xr=f32(far, p.chunks, rows, LANES),
+        sch=f32(m * p.matrix, LANES),
+        cbuf=f32(NB * p.chunk_pitch, LANES),
+        cgrid=f32(NB * p.chunk, LANES),
+        sbuf=f32(far, p.chunks, PLANES * p.chunk, LANES),
+        rbuf=f32(far, p.chunks, PLANES * p.chunk, LANES),
+        xe=f32(NB * p.part_pitch, LANES),
+        xsend=f32(p.parts, PLANES * p.part, LANES),
+        xr=f32(far, p.parts, PLANES * p.part, LANES),
+        fwd=half(p.groups, p.all_modes, 3 * z),
+        back=half(z, 3 * m),
+        far=half(far * p.parts, z, 3 * p.part),
         one=half(LANES, LANES),
         oneT=half(LANES, LANES),
         scale=f32(8, LANES),
+        coef=f32(1, LANES),
+        cell=pltpu.VMEM((1, LANES), jnp.int32),
         keep=f32(NB, LANES),
         weight=f32(NB, LANES),
         xs=f32(ITERS, 2, 2, m, LANES),
@@ -138,22 +155,22 @@
         yh=f32(ITERS, 3, 2, m, LANES),
         ps=f32(ITERS, 1, 2 * m),
         pr=f32(ITERS, p.peers, 1, 2 * m),
-        s_local=dma(5),
+        s_local=dma(7),
         s_halo=dma(2, ITERS, 8),
         s_sum=dma(2, ITERS, p.peers),
-        s_cx=dma(2, far),
-        s_cy=dma(2, far, max(1, p.couple_ways - 1)),
-        s_ix=dma(2, far),
-        s_iy=dma(2, far, max(1, p.inner_ways - 1)),
+        s_couple=dma(2, 2, far, max(1, p.ey - 1)),
+        s_inner=dma(2, 3, far, max(1, p.ex - 1, p.ey - 1)),
         s_f1=dma(2, far, p.chunks),
-        s_f2=dma(2, far),
-        s_b1=dma(2, far, p.chunks),
+        s_f2=dma(2, far, 4),
+        s_b1=dma(2, far, p.parts),
     )
 
 
-def kernel(p, names, forcing, coef_ref, cell_ref, schur_in, couple_in, inner_in, fwd, back_own, back_far, out, *refs):
+def kernel(p, names, forcing, coef_in, cell_in, schur_in, couple_in, inner_in, table, out, *refs):
     s = types.SimpleNamespace(**dict(zip(names, refs)))
     m, z, gm, mc = p.modes, p.planes, p.all_modes, p.chunk
+    mp, gp, cp, nb = p.pitch, p.all_pitch, p.chunk_pitch, p.matrix
+    mo, op = p.part, p.part_pitch
     cells = LANES
     sizes = {"fourier": p.groups, "ex": p.ex, "ey": p.ey}
     place = {axis: lax.axis_index(axis) for axis in sizes}
@@ -177,6 +194,84 @@
     hops = range(1, p.groups)
     around = [(a, b) for a in range(p.ex) for b in range(p.ey) if a or b]
 
+    bottom = lambda k: k
+    top = lambda k: 3 * P_SIZE - k
+    left = lambda k: (NB - k) % NB
+    right = lambda k: P_SIZE + k
+    last = cells - ELY
+
+    def turned(value, shift):
+        shift = shift % cells
+        return pltpu.roll(value, shift, 1) if shift else value
+
+    def grid(rows):
+        where = lax.broadcasted_iota(jnp.int32, (rows, cells), 1)
+        return where // ELY, where % ELY
+
+    def compress(load, store, rows):
+        row, col = grid(rows)
+
+        def sideways(k):
+            return load(left(k)) + jnp.where(row == 0, 0.0, turned(load(right(k)), ELY))
+
+        corner = sideways(P_SIZE)
+        store(0, sideways(0) + jnp.where(col == 0, 0.0, turned(corner, 1)))
+        for k in range(1, P_SIZE):
+            store(k, load(k) + jnp.where(col == 0, 0.0, turned(load(top(k)), 1)))
+            store(P_SIZE - 1 + k, sideways(k))
+        edge = load(right(0)) + jnp.where(col == 0, 0.0, turned(load(right(P_SIZE)), 1))
+        far_row = turned(edge, -last)
+        far_col = turned(corner, 1 - ELY)
+        for k in range(1, P_SIZE):
+            far_row = jnp.where(row == k, turned(load(right(k)), ELY * k - last), far_row)
+            far_col = jnp.where(col == k, turned(load(top(k)), k - ELY + 1), far_col)
+        tip = turned(load(top(P_SIZE)), P_SIZE - ELY + 1)
+        store(2 * P_SIZE - 1, far_row)
+        store(
+            2 * P_SIZE,
+            jnp.where(
+                col < P_SIZE,
+                far_col,
+                jnp.where((col == P_SIZE) & (row == ELX - 1), tip, 0.0),
+            ),
+        )
+
+    def pick_planes(load, store, rows):
+        row, col = grid(rows)
+        far_row = turned(load(right(0)), -last)
+        far_col = turned(load(top(0)), 1 - ELY)
+        for k in range(P_SIZE):
+            store(k, load(k))
+        for k in range(1, P_SIZE):
+            store(P_SIZE - 1 + k, load(left(k)))
+            far_row = jnp.where(row == k, turned(load(right(k)), ELY * k - last), far_row)
+        for k in range(1, P_SIZE + 1):
+            far_col = jnp.where(col == k, turned(load(top(k)), k - ELY + 1), far_col)
+        store(2 * P_SIZE - 1, far_row)
+        store(2 * P_SIZE, far_col)
+
+    def spread(load, n, rows, inside):
+        row, col = grid(rows)
+        if n < P_SIZE:
+            return load(n)
+        if n > 3 * P_SIZE:
+            return load(P_SIZE - 1 + NB - n)
+        if n < 2 * P_SIZE:
+            k = n - P_SIZE
+            beside = turned(load(k and P_SIZE - 1 + k), -ELY) if inside else 0.0
+            return jnp.where(
+                row == ELX - 1, turned(load(2 * P_SIZE - 1), last - ELY * k), beside
+            )
+        k = 3 * P_SIZE - n
+        if inside:
+            above = turned(load(k) if k < P_SIZE else spread(load, P_SIZE, rows, True), -1)
+        else:
+            above = 0.0
+        return jnp.where(col == ELY - 1, turned(load(2 * P_SIZE), ELY - 1 - k), above)
+
+    def planes_of(ref, rows):
+        return lambda k: ref[k * rows : (k + 1) * rows, :]
+
     loads = [
         pltpu.make_async_copy(couple_in, s.cin, s.s_local.at[0]),
         pltpu.make_async_copy(inner_in, s.iin, s.s_local.at[1]),
@@ -185,6 +280,8 @@
         ),
         pltpu.make_async_copy(forcing.at[pl.ds(0, NB)], s.f.at[pl.ds(0, NB)], s.s_local.at[3]),
         pltpu.make_async_copy(schur_in, s.sin, s.s_local.at[4]),
+        pltpu.make_async_copy(coef_in, s.coef, s.s_local.at[5]),
+        pltpu.make_async_copy(cell_in, s.cell, s.s_local.at[6]),
     ]
     for load in loads:
         load.start()
@@ -225,30 +322,44 @@
         )
     pl.semaphore_wait(barrier, len(around) + p.groups - 1)
 
-    def share_out(pack, part, ways, sem_x, sem_y):
-        turn = lax.rem(place["ey"], ways)
-        rows = aligned(turn * part, part) if part % 8 else pl.ds(pl.multiple_of(turn * part, 8), part)
-        across = [
-            remote(
-                pack.at[0, rows], pack.at[g, rows], sem_x, (g - 1,),
-                {"fourier": shifted("fourier", g)},
-            )
-            for g in hops
+    def share_out(pack, part, over_ex, sems):
+        turn = place["ey"] * p.ex + place["ex"] if over_ex else place["ey"]
+        rows = tile(turn * part, part)
+        stages = [
+            [
+                remote(
+                    pack.at[0, rows], pack.at[g, rows], sems, (0, g - 1, 0),
+                    {"fourier": shifted("fourier", g)},
+                )
+                for g in hops
+            ]
         ]
-        beside = [
-            remote(
-                pack.at[g, rows], pack.at[g, rows], sem_y, (g - 1, k - 1),
-                {"ey": place["ey"] - turn + lax.rem(turn + k, ways)},
-            )
-            for g in hops
-            for k in range(1, ways)
-        ]
-        return across, beside
-
-    couple_x, couple_y = share_out(s.cpack, p.couple_part, p.couple_ways, s.s_cx, s.s_cy)
-    inner_x, inner_y = share_out(s.ipack, p.inner_part, p.inner_ways, s.s_ix, s.s_iy)
-    for copy in couple_x:
-        copy.start()
+        for axis in ("ex", "ey") if over_ex else ("ey",):
+            if over_ex and axis == "ey":
+                rows = tile(place["ey"] * p.ex * part, p.ex * part)
+            stages.append(
+                [
+                    remote(
+                        pack.at[g, rows], pack.at[g, rows], sems, (len(stages), g - 1, k - 1),
+                        {axis: shifted(axis, k)},
+                    )
+                    for g in hops
+                    for k in range(1, sizes[axis])
+                ]
+            )
+        return stages
+
+    def start(stage):
+        for copy in stage:
+            copy.start()
+
+    def arrive(stage):
+        for copy in stage:
+            copy.wait_recv()
+
+    couple = share_out(s.cpack, p.couple_part, False, s.s_couple)
+    inner_parts = share_out(s.ipack, p.inner_part, True, s.s_inner)
+    start(couple[0])
 
     loads[1].wait()
     ir = p.inner_rows
@@ -256,16 +367,37 @@
     for i in range(ir):
         picks = [s.iin[min(k * ir + i, NI - 1), :, :] for k in range(p.fold)]
         s.ipack[0, i * TALL : i * TALL + NI, :] = jnp.concatenate(picks, 1)
-    for copy in inner_x:
-        copy.start()
-
+    start(inner_parts[0])
+
+    bounds = [0, NI // 7, NI * 3 // 7, NI * 5 // 7, NI]
+    second = [
+        [
+            remote(
+                forcing.at[pl.ds(NB + a, b - a)], s.fo.at[g - 1, pl.ds(a, b - a)], s.s_f2,
+                (g - 1, k), {"fourier": shifted("fourier", g)},
+            )
+            for g in hops
+        ]
+        for k, (a, b) in enumerate(zip(bounds, bounds[1:]))
+    ]
+    start(second[0])
+
+    for g in range(p.groups):
+        s.fwd[g] = stacked(table[:, g * z : (g + 1) * z])
+    flipped = jnp.transpose(table[...])[:z]
+    s.back[...] = stacked(flipped[:, :m])
+    for k in range((p.groups - 1) * p.parts):
+        s.far[k] = stacked(flipped[:, m + k * mo : m + (k + 1) * mo])
+
+    loads[5].wait()
+    loads[6].wait()
     lines = lax.broadcasted_iota(jnp.int32, (LANES, LANES), 0)
-    hot = jnp.where(lines == cell_ref[0:1, :], 1.0, 0.0).astype(jnp.float32)
+    hot = jnp.where(lines == s.cell[...], 1.0, 0.0).astype(jnp.float32)
     hot_t = jnp.transpose(hot)
     s.oneT[...] = hot.astype(jnp.bfloat16)
     s.one[...] = hot_t.astype(jnp.bfloat16)
     s.scale[...] = lax.dot_general(
-        jnp.broadcast_to(coef_ref[0:1, :], (8, LANES)),
+        jnp.broadcast_to(s.coef[...], (8, LANES)),
         hot_t,
         (((1,), (0,)), ((), ())),
         precision=HIGHEST,
@@ -282,7 +414,7 @@
         for b in range(br):
             turned_rows = flat(s.cpack, g, b, DEEP, br, NI)
             for k in range(p.fold):
-                s.cf[pl.ds(g * m * NB + k * br + b, m, stride=NB), :] = turned_rows[
+                s.cf[pl.ds(g * m * nb + k * br + b, m, stride=nb), :] = turned_rows[
                     k * m : (k + 1) * m
                 ]
 
@@ -296,9 +428,9 @@
                     ]
 
     def spectrum(n):
-        s.spec[aligned(n * gm, gm), :] = dot(fwd[0], pile(s.f[n]))
-
-    clear(s.spec, NODES * gm, (NB + DEEP) * gm)
+        s.spec[tile(n * gp, gm), :] = dot(s.fwd[0], pile(s.f[n]))
+
+    clear(s.spec, NODES * gp, (NB + DEEP) * gp)
     loads[2].wait()
     loop(NI, 7, lambda n: spectrum(NB + n))
     loads[3].wait()
@@ -313,15 +445,19 @@
     def condense(g, c, store):
         def one_mode(k):
             j = g * m + c * mc + k
-            inner = s.spec[pl.ds(NB * gm + j, DEEP, stride=gm), :]
-            matrix = s.cf[aligned(j * NB, NB), :DEEP]
-            s.cbuf[pl.ds(k, NB, stride=mc), :] = s.spec[
-                pl.ds(j, NB, stride=gm), :
+            inner = s.spec[pl.ds(NB * gp + j, DEEP, stride=gp), :]
+            matrix = s.cf[tile(j * nb, NB), :DEEP]
+            s.cbuf[pl.ds(k, NB, stride=cp), :] = s.spec[
+                pl.ds(j, NB, stride=gp), :
             ] - product(matrix, inner)
 
         loop(mc, 8, one_mode)
         for block in range(NB * mc // LANES):
-            store(block, permuted(s.cbuf[block * LANES : (block + 1) * LANES, :], s.one))
+            rows = [
+                s.cbuf[n * cp : n * cp + mc, :]
+                for n in range(block * (LANES // mc), (block + 1) * (LANES // mc))
+            ]
+            store(block, permuted(jnp.concatenate(rows, 0), s.one))
 
     def keep_own(c):
         per = LANES // mc
@@ -329,27 +465,33 @@
         def store(block, rows):
             for k in range(per):
                 n = block * per + k
-                s.res[n * m + c * mc : n * m + (c + 1) * mc, :] = rows[k * mc : (k + 1) * mc]
+                s.res[n * mp + c * mc : n * mp + (c + 1) * mc, :] = rows[k * mc : (k + 1) * mc]
 
         return store
 
-    for copy in couple_x:
-        copy.wait_recv()
-    for copy in couple_y:
-        copy.start()
-    condense(0, 0, keep_own(0))
-    for copy in couple_y:
-        copy.wait_recv()
+    arrive(couple[0])
+    start(couple[1])
+    arrive(inner_parts[0])
+    start(inner_parts[1])
+    early = p.chunks // 2
+    for c in range(early):
+        condense(0, c, keep_own(c))
+    arrive(couple[1])
 
     first = []
     for g in hops:
         couple_matrices(g)
         for c in range(p.chunks):
 
-            def store(block, rows, g=g, c=c):
-                s.sbuf[g - 1, c, block * LANES : (block + 1) * LANES, :] = rows
+            def store(block, rows):
+                s.cgrid[block * LANES : (block + 1) * LANES, :] = rows
 
             condense(g, c, store)
+
+            def put(k, value, g=g, c=c):
+                s.sbuf[g - 1, c, k * mc : (k + 1) * mc, :] = value
+
+            compress(planes_of(s.cgrid, mc), put, mc)
             copy = remote(
                 s.sbuf.at[g - 1, c], s.rbuf.at[g - 1, c], s.s_f1, (g - 1, c),
                 {"fourier": shifted("fourier", -g)},
@@ -357,20 +499,12 @@
             copy.start()
             first.append((g, c, copy))
 
-    second = []
-    for g in hops:
-        copy = remote(
-            forcing.at[pl.ds(NB, NI)], s.fo.at[g - 1], s.s_f2, (g - 1,),
-            {"fourier": shifted("fourier", g)},
-        )
-        copy.start()
-        second.append(copy)
-    for copy in inner_x:
-        copy.wait_recv()
-    for copy in inner_y:
-        copy.start()
-
-    for c in range(1, p.chunks):
+    for stage in second[1:]:
+        start(stage)
+    arrive(inner_parts[1])
+    start(inner_parts[2])
+
+    for c in range(early, p.chunks):
         condense(0, c, keep_own(c))
 
     loads[4].wait()
@@ -380,7 +514,7 @@
         rows = jnp.concatenate([high, high, rows - high, jnp.zeros_like(rows)], 0)
         if m < LANES:
             rows = jnp.concatenate([rows, jnp.zeros((LANES, LANES - m), jnp.float32)], 1)
-        s.sch[pl.ds(a, m, stride=NB), :] = jnp.transpose(rows)[:m]
+        s.sch[pl.ds(a, m, stride=nb), :] = jnp.transpose(rows)[:m]
 
     slots = lax.broadcasted_iota(jnp.int32, (NB, cells), 0)
     places = lax.broadcasted_iota(jnp.int32, (NB, cells), 1)
@@ -395,28 +529,22 @@
     keep = jnp.where(dropped, 0.0, 1.0).astype(jnp.float32)
     s.keep[...] = keep
     s.weight[...] = keep * jnp.where(slots % P_SIZE == 0, 0.25, 0.5)
-    for ref in (s.x, s.dir, s.along):
-        ref[...] = jnp.zeros_like(ref)
 
     def couple_turned(q):
-        square = jnp.transpose(s.cf[aligned(q * LANES, LANES), :])
+        rows = [s.cf[tile((q * (LANES // NB) + k) * nb, NB), :] for k in range(LANES // NB)]
+        square = jnp.transpose(jnp.concatenate(rows, 0))
         for k in range(LANES // NB):
             piece = square[:DEEP] if k == 0 else pltpu.roll(square[:DEEP], LANES - k * NB, 1)
             s.ct[aligned((q * (LANES // NB) + k) * DEEP, DEEP), :] = piece
 
     loop(gm * NB // LANES, 4, couple_turned)
     inner_matrices(0)
-    for copy in inner_y:
-        copy.wait_recv()
+    arrive(inner_parts[2])
     for g in hops:
         inner_matrices(g)
 
     def node(n):
-        return aligned(n * m, m)
-
-    def turned(value, shift):
-        shift = shift % cells
-        return pltpu.roll(value, shift, 1) if shift else value
+        return tile(n * mp, m)
 
     def exists(axis, step):
         if step == 0:
@@ -442,12 +570,7 @@
             lambda: guarded(ex_step, ey_step, copy.wait_send),
         )
 
-    def assemble(ref, turn):
-        bottom = lambda k: k
-        top = lambda k: 3 * P_SIZE - k
-        left = lambda k: (NB - k) % NB
-        right = lambda k: P_SIZE + k
-        last = cells - ELY
+    def assemble(ref, turn, meanwhile):
         copies = []
         up = jnp.zeros((m, cells), jnp.float32)
         down = up
@@ -486,8 +609,9 @@
             ref[node(right(k)), :] = here_right + jnp.where(
                 lane_row == ELX - 1, 0.0, turned(here_left, -ELY)
             )
-        for arrive, _ in copies:
-            arrive()
+        meanwhile()
+        for wait, _ in copies:
+            wait()
 
         for k in range(P_SIZE + 1):
             part, lanes = divmod(k, P_SIZE)
@@ -533,9 +657,9 @@
         scale = s.scale[0:1, :]
 
         def one_mode(k):
-            value = s.res[pl.ds(k, NB, stride=m), :]
-            matrix = s.sch[aligned(k * NB, NB), : 3 * NB].astype(jnp.bfloat16)
-            s.app[pl.ds(k, NB, stride=m), :] = dot(matrix, pile(value)) * scale
+            value = s.res[pl.ds(k, NB, stride=mp), :]
+            matrix = s.sch[tile(k * nb, NB), : 3 * NB].astype(jnp.bfloat16)
+            s.app[pl.ds(k, NB, stride=mp), :] = dot(matrix, pile(value)) * scale
 
         loop(m, 8, one_mode)
 
@@ -587,125 +711,147 @@
     for g, c, copy in first:
         copy.wait_recv()
 
-        def add(n, g=g, c=c):
-            rows = aligned(n * m + c * mc, mc)
-            s.res[rows, :] = s.res[rows, :] + s.rbuf[g - 1, c, aligned(n * mc, mc), :]
-
-        loop(NB, 8, add)
-    assemble(s.res, 0)
-
-    def scalars(turn, norm, curve, norm_before, step_before):
-        ratio = jnp.where(turn == 0, 0.0, norm / norm_before)
-        return ratio, norm / (curve - ratio * norm / step_before)
-
-    def sweep(turn, carry):
+        arrived = planes_of(s.rbuf.at[g - 1, c], mc)
+        for n in range(NB):
+            rows = pl.ds(n * mp + c * mc, mc)
+            s.res[rows, :] = s.res[rows, :] + spread(arrived, n, mc, False)
+
+    def add_far(piece):
+        def one_node(i):
+            n = bounds[piece] + i
+            rows = tile((NB + n) * gp, gm)
+            total = s.spec[rows, :]
+            for g in hops:
+                total = total + dot(s.fwd[g], pile(s.fo[g - 1, n]))
+            s.spec[rows, :] = total
+
+        arrive(second[piece])
+        loop(bounds[piece + 1] - bounds[piece], 7, one_node)
+
+    assemble(s.res, 0, lambda: add_far(0))
+
+    carry = None
+    for turn in range(ITERS):
         operator()
         copies = sums_start(turn)
-        assemble(s.app, turn + 1)
+        if turn < ITERS - 1:
+            assemble(s.app, turn + 1, (lambda: add_far(1)) if turn else (lambda: None))
+        else:
+            add_far(2)
         norm, curve = sums_end(turn, copies)
-        ratio, step_size = scalars(turn, norm, curve, *carry)
-
-        def update(n):
+        if turn == 0:
+            step_size = norm / curve
+        else:
+            ratio = norm / carry[0]
+            step_size = norm / (curve - ratio * norm / carry[1])
+        carry = norm, step_size
+
+        def update(n, turn=turn):
             rows = node(n)
-            search = s.res[rows, :] + ratio * s.dir[rows, :]
-            along = s.app[rows, :] + ratio * s.along[rows, :]
-            s.x[rows, :] = s.x[rows, :] + step_size * search
-            s.dir[rows, :] = search
-            s.along[rows, :] = along
-            s.res[rows, :] = s.res[rows, :] - step_size * along
+            search, along = s.res[rows, :], s.app[rows, :]
+            residual = search
+            if turn:
+                search = search + ratio * s.dir[rows, :]
+                s.x[rows, :] = s.x[rows, :] + step_size * search
+            else:
+                s.x[rows, :] = step_size * search
+            if turn < ITERS - 1:
+                if turn:
+                    along = along + ratio * s.along[rows, :]
+                s.dir[rows, :] = search
+                s.along[rows, :] = along
+                s.res[rows, :] = residual - step_size * along
 
         loop(NB, 4, update)
-        return norm, step_size
-
-    one = jnp.ones((m, 1), jnp.float32)
-    carry = lax.fori_loop(0, ITERS - 1, sweep, (one, one))
-    operator()
-    norm, curve = sums_end(ITERS - 1, sums_start(ITERS - 1))
-    ratio, step_size = scalars(ITERS - 1, norm, curve, *carry)
-
-    def finish(n):
-        rows = node(n)
-        s.x[rows, :] = s.x[rows, :] + step_size * (s.res[rows, :] + ratio * s.dir[rows, :])
-
-    loop(NB, 4, finish)
-
-    per = LANES // mc
+
+    def solved(c):
+        return lambda n: s.x[n * mp + c * mo : n * mp + (c + 1) * mo, :]
+
     third = []
-    for c in range(p.chunks):
-        for block in range(NB // per):
-            rows = jnp.concatenate(
-                [
-                    s.x[n * m + c * mc : n * m + (c + 1) * mc, :]
-                    for n in range(block * per, (block + 1) * per)
-                ],
-                0,
-            )
-            s.xe[c, block * LANES : (block + 1) * LANES, :] = permuted(rows, s.oneT)
+    for c in range(p.parts):
+
+        def put(k, value, c=c):
+            s.xsend[c, k * mo : (k + 1) * mo, :] = value
+
+        pick_planes(solved(c), put, mo)
         for g in hops:
             copy = remote(
-                s.xe.at[c], s.xr.at[g - 1, c], s.s_b1, (g - 1, c),
+                s.xsend.at[c], s.xr.at[g - 1, c], s.s_b1, (g - 1, c),
                 {"fourier": shifted("fourier", g)},
             )
             copy.start()
             third.append((g, c, copy))
 
-    for copy in second:
-        copy.wait_recv()
-
-    def add_far(n):
-        rows = aligned((NB + n) * gm, gm)
-        total = s.spec[rows, :]
-        for g in hops:
-            total = total + dot(fwd[g], pile(s.fo[g - 1, n]))
-        s.spec[rows, :] = total
-
-    loop(NI, 7, add_far)
-    inverse_coef = 1.0 / coef_ref[0:1, :]
-
-    def base(j):
-        inner = s.spec[pl.ds(NB * gm + j, DEEP, stride=gm), :]
-        matrix = s.invf[pl.ds(pl.multiple_of(j * TALL, 8), TALL), :DEEP]
-        value = product(matrix, inner) * inverse_coef
-        s.spec[pl.ds(NB * gm + j, NI, stride=gm), :] = value[:NI]
-
-    loop(gm, 4, base)
-
-    def place_cycle(g, c, source):
-        def interior(k):
-            j = g * m + c * mc + k
-            matrix = s.ct[aligned(j * DEEP, DEEP), :NB]
-            value = product(matrix, source[pl.ds(k, NB, stride=mc), :])
-            rows = pl.ds(NB * gm + j, NI, stride=gm)
-            s.spec[rows, :] = s.spec[rows, :] - value[:NI]
-
-        loop(mc, 4, interior)
-
-        def cycle(n):
-            s.spec[aligned(n * gm + g * m + c * mc, mc), :] = source[aligned(n * mc, mc), :]
-
-        loop(NB, 8, cycle)
-
-    for c in range(p.chunks):
-        place_cycle(0, c, s.xe.at[c])
+    for copies in couple + inner_parts + second:
+        for copy in copies:
+            copy.wait_send()
+    for _, _, copy in first:
+        copy.wait_send()
+
+    for piece in range(3, len(second)):
+        add_far(piece)
+    inverse_coef = 1.0 / s.coef[...]
+
+    def restore(g, c, load):
+        per = LANES // mo
+        for block in range(NB // per):
+            nodes = range(block * per, (block + 1) * per)
+            rows = permuted(jnp.concatenate([load(n) for n in nodes], 0), s.oneT)
+            for k, n in enumerate(nodes):
+                piece = rows[k * mo : (k + 1) * mo]
+                s.xe[n * op : n * op + mo, :] = piece
+                start_row = n * gp + g * m + c * mo
+                s.spec[start_row : start_row + mo, :] = piece
+
+    def from_inner(j):
+        inner = s.spec[pl.ds(NB * gp + j, DEEP, stride=gp), :]
+        matrix = s.invf[tile(j * TALL, TALL), :DEEP]
+        return product(matrix, inner) * inverse_coef
+
+    def from_cycle(j, k):
+        matrix = s.ct[tile(j * DEEP, TALL), :NB]
+        return product(matrix, s.xe[pl.ds(k, NB, stride=op), :])
+
+    def inner_rows(j):
+        return pl.ds(NB * gp + j, NI, stride=gp)
+
+    for c in range(p.parts):
+        restore(0, c, solved(c))
+
+        def own_mode(k, c=c):
+            j = c * mo + k
+            s.spec[inner_rows(j), :] = (from_inner(j) - from_cycle(j, k))[:NI]
+
+        loop(mo, 8, own_mode)
 
     def own_velocity(n):
-        out[n] = dot(back_own[...], pile(s.spec[aligned(n * gm, m), :]))
+        out[n] = dot(s.back[...], pile(s.spec[tile(n * gp, m), :]))
 
     loop(NODES, 9, own_velocity)
+
+    def base(k):
+        s.spec[inner_rows(m + k), :] = from_inner(m + k)[:NI]
+
+    loop(gm - m, 8, base)
 
     for g, c, copy in third:
         copy.wait_recv()
-        place_cycle(g, c, s.xr.at[g - 1, c])
+        arrived = planes_of(s.xr.at[g - 1, c], mo)
+        restore(g, c, lambda n, arrived=arrived: spread(arrived, n, mo, True))
+
+        def far_mode(k, g=g, c=c):
+            j = g * m + c * mo + k
+            s.spec[inner_rows(j), :] = s.spec[inner_rows(j), :] - from_cycle(j, k)[:NI]
+
+        loop(mo, 8, far_mode)
 
         def far_velocity(n, g=g, c=c):
-            rows = s.spec[aligned(n * gm + g * m + c * mc, mc), :]
-            out[n] = out[n] + dot(back_far[(g - 1) * p.chunks + c], pile(rows))
+            rows = s.spec[tile(n * gp + g * m + c * mo, mo), :]
+            out[n] = out[n] + dot(s.far[(g - 1) * p.parts + c], pile(rows))
 
         loop(NODES, 9, far_velocity)
 
-    for copy in couple_x + couple_y + inner_x + inner_y + second:
-        copy.wait_send()
-    for _, _, copy in first + third:
+    for _, _, copy in third:
         copy.wait_send()
 
 
@@ -717,48 +863,33 @@
     me = lax.axis_index("fourier")
     length = planes * p.groups
 
-    def group_of(hop):
-        return lax.rem(me + p.groups - hop, p.groups)
-
-    def iota(shape, dim):
-        return lax.broadcasted_iota(jnp.int32, shape, dim)
-
-    dims = (p.groups, p.all_modes, planes)
-    mode = group_of(iota(dims, 1) // modes) * modes + iota(dims, 1) % modes
-    plane = group_of(iota(dims, 0)) * planes + iota(dims, 2)
-    fwd = stacked_table(dft_values(mode, plane, length))
-    dims = (planes, modes)
-    back_own = stacked_table(
-        dft_values(me * modes + iota(dims, 1), me * planes + iota(dims, 0), length)
-    )
-    dims = ((p.groups - 1) * p.chunks, planes, p.chunk)
-    hop = 1 + iota(dims, 0) // p.chunks
-    mode = group_of(hop) * modes + iota(dims, 0) % p.chunks * p.chunk + iota(dims, 2)
-    back_far = stacked_table(dft_values(mode, me * planes + iota(dims, 1), length))
-
+    def ordered(dim, size):
+        place = lax.broadcasted_iota(jnp.int32, (length, length), dim)
+        return lax.rem(me + p.groups - place // size, p.groups) * size + place % size
+
+    table = dft_values(ordered(0, modes), ordered(1, planes), length)
+    pinned = lambda value: pltpu.with_memory_space_constraint(value, pltpu.HBM)
     scratch = layout(p)
     whole = pl.BlockSpec(memory_space=pltpu.VMEM)
-    stay = pl.BlockSpec(memory_space=pl.ANY)
+    stay = pl.BlockSpec(memory_space=pltpu.HBM)
     velocity = pl.pallas_call(
         functools.partial(kernel, p, tuple(scratch)),
         out_shape=jax.ShapeDtypeStruct((NODES, planes, elements), jnp.float32),
-        in_specs=[stay, whole, whole, stay, stay, stay, whole, whole, whole],
+        in_specs=[stay] * 6 + [whole],
         out_specs=whole,
         scratch_shapes=list(scratch.values()),
         compiler_params=pltpu.CompilerParams(
-            collective_id=0, has_side_effects=True, vmem_limit_bytes=60 << 20
+            collective_id=0, has_side_effects=True, vmem_limit_bytes=44 << 20
         ),
         cost_estimate=pl.CostEstimate(flops=10**9, bytes_accessed=2 * 10**8, transcendentals=0),
     )(
-        jnp.transpose(forcing, (1, 0, 2)),
-        element_coef[None],
-        element_cell[None],
-        jnp.transpose(schur, (1, 2, 0)),
-        jnp.transpose(couple, (2, 1, 0)),
-        jnp.transpose(inner_inv, (1, 2, 0)),
-        fwd,
-        back_own,
-        back_far,
+        pinned(jnp.transpose(forcing, (1, 0, 2))),
+        pinned(element_coef[None]),
+        pinned(element_cell[None]),
+        pinned(jnp.transpose(schur, (1, 2, 0))),
+        pinned(jnp.transpose(couple, (2, 1, 0))),
+        pinned(jnp.transpose(inner_inv, (1, 2, 0))),
+        table,
     )
     return jnp.transpose(velocity, (1, 0, 2))
 

time: 116 us -> 80.8 us (0.70)
  Pallas kernels: 109 us -> 78.1 us
  other arithmetic: 3.93 us -> 0.5 us
  local copies, waits for them, and re-layouts: 3.59 us -> 1.5 us
    pallas_call x1, Pallas kernels: 109 us -> 78.1 us  [on_device(): pl.pallas_call(functools.partial(kernel, p, tuple(scratch)), out_shape=ja...]
    concatenate x3 -> x0, other arithmetic: 2.19 us -> none  [stacked_table(): return jnp.concatenate([high, high, low], -1).astype(jnp.bfloat16)]
    unnamed x1, local copies, waits for them, and re-layouts: 3.59 us -> 1.5 us
    another operation x3 -> x0, other arithmetic: 1.61 us -> none
where the time goes in v2:
time: 80.8 us; the launch traced here: 80.1 us
  Pallas kernels  78.1 us (97%)
  local copies, waits for them, and re-layouts  1.5 us (2%)
    pallas_call x1, Pallas kernels, on_device(): pl.pallas_call(functools.partial(kernel, p, tuple(scratch)), out_shape=ja...  78.1 us

profile of v2, /device:TPU:0, one launch (start us, length us, event | category | flops | bytes accessed | tf_op | source)
XLA Modules:
  0.0 80.1 jit_solution(6088307809886621771)
XLA Ops:
  0.0 0.5 select_select_fusion.table
  0.5 78.1 %shard_map.64 = f32[81,64,128]{2,1,0:T(8,128)S(1)} custom-call(f32[81,64,128]{2,1,0:T(8,128)} %bitcast.8, f32[1,128]{1,0:T(1,128)} %bitcast.12, s32[1,128]{1,0:T(1,128)} %bitcast.13, f32[32,32,64]{2,1,0:T(8,128)} %bitcast.11, f32[49,32,64]{2,1,0:T(8,128)} %bitcast.10, f32[49,49,64]{2,1,0:T(8,128)} %bitcast.9, f32[128,128]{1,0:T(8,128)S(1)} %select_select_fusion.table), custom_call_target="tpu_custom_call" | custom-call | flops 1000000000 | bytes 200000000 | tf_op jit(solution)/shard_map/pallas_call | solution.py:875
  78.6 1.5 %copy.8 = f32[64,81,128]{2,0,1:T(8,128)} copy(f32[64,81,128]{2,0,1:T(8,128)S(1)} %bitcast.7) | data formatting | bytes 5308416
  (3 shorter events, 0.0 us)

commit v3 on v2

--- a/solution.py
+++ b/solution.py
@@ -17,8 +17,9 @@
 NI = (P_SIZE - 1) ** 2
 NODES = NB + NI
 DEEP = 64
-TALL = 56
+TALL = 64
 LANES = 128
+WIDE = 256
 PLANES = 2 * P_SIZE + 1
 HIGHEST = lax.Precision.HIGHEST
 
@@ -61,6 +62,18 @@
     return jnp.concatenate([high, low, high], 0)
 
 
+def apply_table(table, values):
+    result = dot(table, jnp.concatenate([pile(value) for value in values], 1))
+    return [result[:, k * LANES : (k + 1) * LANES] for k in range(len(values))]
+
+
+def pairs(start, stop, unroll, body):
+    count = (stop - start) // 2
+    loop(count, unroll, lambda i: body([start + 2 * i, start + 2 * i + 1]))
+    if (stop - start) % 2:
+        body([stop - 1])
+
+
 def aligned(start, size):
     return pl.ds(start if isinstance(start, int) else pl.multiple_of(start, size), size)
 
@@ -90,10 +103,12 @@
         self.chunks = modes // self.chunk
         self.part = min(32, modes)
         self.parts = modes // self.part
-        self.part_pitch = self.part + 8
         self.fold = max(1, LANES // modes)
         self.couple_rows = NB // self.fold
-        self.couple_ways = self.ey
+        self.couple_bits = 2
+        while self.ey % 2**self.couple_bits:
+            self.couple_bits -= 1
+        self.couple_ways = 2**self.couple_bits
         step = 8 * self.couple_ways
         self.couple_part = -(-NI * self.couple_rows // step) * 8
         self.couple_all = max(DEEP * self.couple_rows, self.couple_part * self.couple_ways)
@@ -129,14 +144,12 @@
         cpack=f32(p.groups, p.couple_all, LANES),
         ipack=f32(p.groups, p.inner_all, LANES),
         cf=f32(p.all_modes * p.matrix, LANES),
-        ct=f32(p.all_modes * DEEP, LANES),
         invf=f32(p.all_modes * TALL, LANES),
         sch=f32(m * p.matrix, LANES),
         cbuf=f32(NB * p.chunk_pitch, LANES),
         cgrid=f32(NB * p.chunk, LANES),
         sbuf=f32(far, p.chunks, PLANES * p.chunk, LANES),
         rbuf=f32(far, p.chunks, PLANES * p.chunk, LANES),
-        xe=f32(NB * p.part_pitch, LANES),
         xsend=f32(p.parts, PLANES * p.part, LANES),
         xr=f32(far, p.parts, PLANES * p.part, LANES),
         fwd=half(p.groups, p.all_modes, 3 * z),
@@ -153,12 +166,12 @@
         xh=f32(ITERS, 2, 2, m, LANES),
         ys=f32(ITERS, 2, m, LANES),
         yh=f32(ITERS, 3, 2, m, LANES),
-        ps=f32(ITERS, 1, 2 * m),
+        ps=f32(ITERS, p.peers, 1, 2 * m),
         pr=f32(ITERS, p.peers, 1, 2 * m),
         s_local=dma(7),
         s_halo=dma(2, ITERS, 8),
-        s_sum=dma(2, ITERS, p.peers),
-        s_couple=dma(2, 2, far, max(1, p.ey - 1)),
+        s_sum=dma(2, ITERS),
+        s_couple=dma(2, 1 + p.couple_bits, far, 1),
         s_inner=dma(2, 3, far, max(1, p.ex - 1, p.ey - 1)),
         s_f1=dma(2, far, p.chunks),
         s_f2=dma(2, far, 4),
@@ -170,7 +183,7 @@
     s = types.SimpleNamespace(**dict(zip(names, refs)))
     m, z, gm, mc = p.modes, p.planes, p.all_modes, p.chunk
     mp, gp, cp, nb = p.pitch, p.all_pitch, p.chunk_pitch, p.matrix
-    mo, op = p.part, p.part_pitch
+    mo = p.part
     cells = LANES
     sizes = {"fourier": p.groups, "ex": p.ex, "ey": p.ey}
     place = {axis: lax.axis_index(axis) for axis in sizes}
@@ -283,8 +296,8 @@
         pltpu.make_async_copy(coef_in, s.coef, s.s_local.at[5]),
         pltpu.make_async_copy(cell_in, s.cell, s.s_local.at[6]),
     ]
-    for load in loads:
-        load.start()
+    for k in (0, 2, 3, 5, 6, 1, 4):
+        loads[k].start()
 
     s.xh[...] = jnp.zeros_like(s.xh)
     s.yh[...] = jnp.zeros_like(s.yh)
@@ -309,6 +322,9 @@
         if stop > start:
             ref[pl.ds(start, stop - start), :] = jnp.zeros((stop - start, LANES), jnp.float32)
 
+    for g in range(p.groups):
+        s.fwd[g] = stacked(table[:, g * z : (g + 1) * z])
+
     br = p.couple_rows
     own_rows = NI * br
     got_rows = p.couple_part * p.couple_ways
@@ -322,8 +338,30 @@
         )
     pl.semaphore_wait(barrier, len(around) + p.groups - 1)
 
-    def share_out(pack, part, over_ex, sems):
-        turn = place["ey"] * p.ex + place["ex"] if over_ex else place["ey"]
+    def share_by_halves(pack, part, sems):
+        stages, bits = [], p.couple_bits
+        digit = [place["ey"] // 2**k % 2 for k in range(bits)]
+        turn = sum(digit[k] * 2 ** (bits - 1 - k) for k in range(bits))
+        for stage in range(bits + 1):
+            held = 2 ** max(0, stage - 1)
+            rows = tile(turn // held * (held * part), held * part)
+            if stage:
+                flip = 2 ** (bits - stage)
+                other = {"ey": place["ey"] + flip * (1 - 2 * digit[bits - stage])}
+            stages.append(
+                [
+                    remote(
+                        pack.at[g if stage else 0, rows], pack.at[g, rows], sems,
+                        (stage, g - 1, 0),
+                        other if stage else {"fourier": shifted("fourier", g)},
+                    )
+                    for g in hops
+                ]
+            )
+        return stages
+
+    def share_out(pack, part, sems):
+        turn = place["ey"] * p.ex + place["ex"]
         rows = tile(turn * part, part)
         stages = [
             [
@@ -334,8 +372,8 @@
                 for g in hops
             ]
         ]
-        for axis in ("ex", "ey") if over_ex else ("ey",):
-            if over_ex and axis == "ey":
+        for axis in ("ex", "ey"):
+            if axis == "ey":
                 rows = tile(place["ey"] * p.ex * part, p.ex * part)
             stages.append(
                 [
@@ -357,19 +395,11 @@
         for copy in stage:
             copy.wait_recv()
 
-    couple = share_out(s.cpack, p.couple_part, False, s.s_couple)
-    inner_parts = share_out(s.ipack, p.inner_part, True, s.s_inner)
+    couple = share_by_halves(s.cpack, p.couple_part, s.s_couple)
+    inner_parts = share_out(s.ipack, p.inner_part, s.s_inner)
     start(couple[0])
 
-    loads[1].wait()
-    ir = p.inner_rows
-    clear(s.ipack.at[0], 0, p.inner_all)
-    for i in range(ir):
-        picks = [s.iin[min(k * ir + i, NI - 1), :, :] for k in range(p.fold)]
-        s.ipack[0, i * TALL : i * TALL + NI, :] = jnp.concatenate(picks, 1)
-    start(inner_parts[0])
-
-    bounds = [0, NI // 7, NI * 3 // 7, NI * 5 // 7, NI]
+    bounds = [0, 8, 22, 36, NI]
     second = [
         [
             remote(
@@ -382,12 +412,40 @@
     ]
     start(second[0])
 
-    for g in range(p.groups):
-        s.fwd[g] = stacked(table[:, g * z : (g + 1) * z])
-    flipped = jnp.transpose(table[...])[:z]
-    s.back[...] = stacked(flipped[:, :m])
-    for k in range((p.groups - 1) * p.parts):
-        s.far[k] = stacked(flipped[:, m + k * mo : m + (k + 1) * mo])
+    def flat(pack, g, start, count, stride, width):
+        rows = pack[g, pl.ds(start, count, stride=stride) if stride > 1 else pl.ds(start, count), :]
+        if count < LANES:
+            rows = jnp.concatenate([rows, jnp.zeros((LANES - count, LANES), jnp.float32)], 0)
+        return jnp.transpose(rows)
+
+    def couple_matrices(g):
+        for b in range(br):
+            turned_rows = flat(s.cpack, g, b, DEEP, br, NI)
+            for k in range(p.fold):
+                s.cf[pl.ds(g * m * nb + k * br + b, m, stride=nb), :] = turned_rows[
+                    k * m : (k + 1) * m
+                ]
+
+    def inner_matrices(g):
+        for i in range(ir):
+            turned_rows = flat(s.ipack, g, i * TALL, TALL, 1, NI)
+            for k in range(p.fold):
+                if k * ir + i < TALL:
+                    s.invf[pl.ds(g * m * TALL + k * ir + i, m, stride=TALL), :] = turned_rows[
+                        k * m : (k + 1) * m
+                    ]
+
+    def spectrum(nodes):
+        values = apply_table(s.fwd[0], [s.f[n] for n in nodes])
+        for n, value in zip(nodes, values):
+            s.spec[tile(n * gp, gm), :] = value
+
+    clear(s.spec, NODES * gp, (NB + DEEP) * gp)
+    loads[2].wait()
+    pairs(NB, NODES, 4, spectrum)
+    loads[3].wait()
+    pairs(0, NB, 4, spectrum)
+    couple_matrices(0)
 
     loads[5].wait()
     loads[6].wait()
@@ -404,42 +462,8 @@
         preferred_element_type=jnp.float32,
     )
 
-    def flat(pack, g, start, count, stride, width):
-        rows = pack[g, pl.ds(start, count, stride=stride) if stride > 1 else pl.ds(start, count), :]
-        if count < LANES:
-            rows = jnp.concatenate([rows, jnp.zeros((LANES - count, LANES), jnp.float32)], 0)
-        return jnp.transpose(rows)
-
-    def couple_matrices(g):
-        for b in range(br):
-            turned_rows = flat(s.cpack, g, b, DEEP, br, NI)
-            for k in range(p.fold):
-                s.cf[pl.ds(g * m * nb + k * br + b, m, stride=nb), :] = turned_rows[
-                    k * m : (k + 1) * m
-                ]
-
-    def inner_matrices(g):
-        for i in range(ir):
-            turned_rows = flat(s.ipack, g, i * TALL, TALL, 1, NI)
-            for k in range(p.fold):
-                if k * ir + i < TALL:
-                    s.invf[pl.ds(g * m * TALL + k * ir + i, m, stride=TALL), :] = turned_rows[
-                        k * m : (k + 1) * m
-                    ]
-
-    def spectrum(n):
-        s.spec[tile(n * gp, gm), :] = dot(s.fwd[0], pile(s.f[n]))
-
-    clear(s.spec, NODES * gp, (NB + DEEP) * gp)
-    loads[2].wait()
-    loop(NI, 7, lambda n: spectrum(NB + n))
-    loads[3].wait()
-    loop(NB, 8, spectrum)
-    couple_matrices(0)
-
     def permuted(rows, hot_ref):
-        high, low = split(rows)
-        both = dot(jnp.concatenate([high, low], 0), hot_ref[...])
+        both = dot(jnp.concatenate(split(rows), 0), hot_ref[...])
         return both[: rows.shape[0]] + both[rows.shape[0] :]
 
     def condense(g, c, store):
@@ -451,16 +475,14 @@
                 pl.ds(j, NB, stride=gp), :
             ] - product(matrix, inner)
 
-        loop(mc, 8, one_mode)
-        for block in range(NB * mc // LANES):
-            rows = [
-                s.cbuf[n * cp : n * cp + mc, :]
-                for n in range(block * (LANES // mc), (block + 1) * (LANES // mc))
-            ]
+        loop(mc, 16, one_mode)
+        per = WIDE // mc
+        for block in range(NB // per):
+            rows = [s.cbuf[n * cp : n * cp + mc, :] for n in range(block * per, (block + 1) * per)]
             store(block, permuted(jnp.concatenate(rows, 0), s.one))
 
     def keep_own(c):
-        per = LANES // mc
+        per = WIDE // mc
 
         def store(block, rows):
             for k in range(per):
@@ -469,14 +491,34 @@
 
         return store
 
+    own_chunks = list(range(p.chunks))
+
+    def condense_own():
+        if own_chunks:
+            c = own_chunks.pop(0)
+            condense(0, c, keep_own(c))
+
     arrive(couple[0])
-    start(couple[1])
+    for copies in couple[1:2]:
+        start(copies)
+    condense_own()
+    loads[1].wait()
+    ir = p.inner_rows
+    clear(s.ipack.at[0], 0, p.inner_all)
+    for i in range(ir):
+        picks = [s.iin[min(k * ir + i, NI - 1), :, :] for k in range(p.fold)]
+        s.ipack[0, i * TALL : i * TALL + NI, :] = jnp.concatenate(picks, 1)
+    start(inner_parts[0])
+
+    for stage, copies in enumerate(couple[2:]):
+        if stage == 0:
+            condense_own()
+        arrive(couple[stage + 1])
+        start(copies)
+    condense_own()
     arrive(inner_parts[0])
     start(inner_parts[1])
-    early = p.chunks // 2
-    for c in range(early):
-        condense(0, c, keep_own(c))
-    arrive(couple[1])
+    arrive(couple[-1])
 
     first = []
     for g in hops:
@@ -484,7 +526,7 @@
         for c in range(p.chunks):
 
             def store(block, rows):
-                s.cgrid[block * LANES : (block + 1) * LANES, :] = rows
+                s.cgrid[block * WIDE : (block + 1) * WIDE, :] = rows
 
             condense(g, c, store)
 
@@ -504,17 +546,29 @@
     arrive(inner_parts[1])
     start(inner_parts[2])
 
-    for c in range(early, p.chunks):
-        condense(0, c, keep_own(c))
+    while own_chunks:
+        condense_own()
+
+    flipped = jnp.transpose(table[...])[:z]
+    s.back[...] = stacked(flipped[:, :m])
+    for k in range((p.groups - 1) * p.parts):
+        s.far[k] = stacked(flipped[:, m + k * mo : m + (k + 1) * mo])
 
     loads[4].wait()
-    for a in range(NB):
-        rows = s.sin[a]
-        high = rows.astype(jnp.bfloat16).astype(jnp.float32)
-        rows = jnp.concatenate([high, high, rows - high, jnp.zeros_like(rows)], 0)
+    group = LANES // NB
+    for q in range(NB // group):
+        rows = jnp.concatenate([s.sin[q * group + k] for k in range(group)], 0)
         if m < LANES:
             rows = jnp.concatenate([rows, jnp.zeros((LANES, LANES - m), jnp.float32)], 1)
-        s.sch[pl.ds(a, m, stride=nb), :] = jnp.transpose(rows)[:m]
+        square = jnp.transpose(rows)[:m]
+        high = square.astype(jnp.bfloat16).astype(jnp.float32)
+        low = square - high
+        where = lax.broadcasted_iota(jnp.int32, (m, LANES), 1)
+        for k in range(group):
+            first_half = jnp.where(where < NB, turned(high, -k * NB), turned(high, NB - k * NB))
+            s.sch[pl.ds(q * group + k, m, stride=nb), :] = jnp.where(
+                where < 2 * NB, first_half, turned(low, 2 * NB - k * NB)
+            )
 
     slots = lax.broadcasted_iota(jnp.int32, (NB, cells), 0)
     places = lax.broadcasted_iota(jnp.int32, (NB, cells), 1)
@@ -530,18 +584,27 @@
     s.keep[...] = keep
     s.weight[...] = keep * jnp.where(slots % P_SIZE == 0, 0.25, 0.5)
 
-    def couple_turned(q):
-        rows = [s.cf[tile((q * (LANES // NB) + k) * nb, NB), :] for k in range(LANES // NB)]
-        square = jnp.transpose(jnp.concatenate(rows, 0))
-        for k in range(LANES // NB):
-            piece = square[:DEEP] if k == 0 else pltpu.roll(square[:DEEP], LANES - k * NB, 1)
-            s.ct[aligned((q * (LANES // NB) + k) * DEEP, DEEP), :] = piece
-
-    loop(gm * NB // LANES, 4, couple_turned)
+    def couple_beside(q):
+        group = LANES // NB
+        rows = [s.cf[tile((q * group + k) * nb, NB), :] for k in range(group)]
+        square = jnp.transpose(jnp.concatenate(rows, 0))[:TALL]
+        where = lax.broadcasted_iota(jnp.int32, (TALL, LANES), 1)
+        for k in range(group):
+            place_rows = tile((q * group + k) * TALL, TALL)
+            s.invf[place_rows, :] = jnp.where(
+                (where >= DEEP) & (where < DEEP + NB),
+                -turned(square, DEEP - k * NB),
+                s.invf[place_rows, :],
+            )
+
     inner_matrices(0)
-    arrive(inner_parts[2])
-    for g in hops:
-        inner_matrices(g)
+
+    def far_matrices():
+        arrive(inner_parts[2])
+        for g in hops:
+            inner_matrices(g)
+
+    fillers = [far_matrices, lambda: loop(gm * NB // LANES, 4, couple_beside)]
 
     def node(n):
         return tile(n * mp, m)
@@ -572,11 +635,14 @@
 
     def assemble(ref, turn, meanwhile):
         copies = []
-        up = jnp.zeros((m, cells), jnp.float32)
-        down = up
+        up = down = None
         for k in range(P_SIZE + 1):
-            up = jnp.where(lane_col == k, turned(ref[node(top(k)), :], k - ELY + 1), up)
-            down = jnp.where(lane_col == k, turned(ref[node(bottom(k)), :], k), down)
+            ends = jnp.where(lane_col == ELY - 1, ref[node(top(k)), :], ref[node(bottom(k)), :])
+            ends = turned(ends, k)
+            up = ends if k == 0 else jnp.where(lane_col == k - 1, ends, up)
+            down = ends if k == 0 else jnp.where(lane_col == k, ends, down)
+        up = jnp.where(lane_col <= P_SIZE, turned(up, 1 - ELY), 0.0)
+        down = jnp.where(lane_col <= P_SIZE, down, 0.0)
         s.ys[turn, 0] = up
         s.ys[turn, 1] = down
         for slot, ex_step in ((1, 1), (2, -1), (0, 0)):
@@ -587,11 +653,12 @@
                         ex_step, ey_step,
                     )
                 )
-        up = jnp.zeros((m, cells), jnp.float32)
-        down = up
         for k in range(P_SIZE):
-            up = jnp.where(lane_row == k, turned(ref[node(right(k)), :], ELY * k - last), up)
-            down = jnp.where(lane_row == k, turned(ref[node(left(k)), :], ELY * k), down)
+            ends = jnp.where(lane_row == ELX - 1, ref[node(right(k)), :], ref[node(left(k)), :])
+            ends = turned(ends, ELY * k)
+            up = ends if k == 0 else jnp.where(lane_row == k - 1, ends, up)
+            down = ends if k == 0 else jnp.where(lane_row == k, ends, down)
+        up = turned(up, -last)
         s.xs[turn, 0, 0] = up
         s.xs[turn, 1, 0] = down
         s.xs[turn, 0, 1] = turned(ref[node(right(P_SIZE)), :], -last)
@@ -615,8 +682,14 @@
 
         for k in range(P_SIZE + 1):
             part, lanes = divmod(k, P_SIZE)
-            low = turned(s.xh[turn, 0, part], -ELY * lanes)
-            high = turned(s.xh[turn, 1, part], last - ELY * lanes)
+            if part:
+                low = s.xh[turn, 0, part]
+                high = turned(s.xh[turn, 1, part], last)
+            else:
+                if k == 0:
+                    from_low, from_high = s.xh[turn, 0, 0], turned(s.xh[turn, 1, 0], last)
+                low = turned(jnp.where(lane_row == k, from_low, from_high), -ELY * k)
+                high = low
             for n, halo, row in ((left(k), low, 0), (right(k), high, ELX - 1)):
                 value = ref[node(n), :] + jnp.where(lane_row == row, halo, 0.0)
                 if n % (2 * P_SIZE) > P_SIZE:
@@ -636,19 +709,16 @@
                 line
                 + jnp.where(lane_col == 0, before, jnp.where(lane_col == P_SIZE, after, 0.0))
             )
-        low_all, high_all = lines
+        low_all, high_all = lines[0], turned(lines[1], ELY - 1)
         for k in range(P_SIZE + 1):
             b, t = bottom(k), top(k)
             here_bottom, here_top = ref[node(b), :], ref[node(t), :]
+            ends = turned(jnp.where(lane_col == k, low_all, high_all), -k)
             ref[node(b), :] = s.keep[b : b + 1, :] * (
-                here_bottom
-                + jnp.where(lane_col == 0, turned(low_all, -k), turned(here_top, 1))
+                here_bottom + jnp.where(lane_col == 0, ends, turned(here_top, 1))
             )
             ref[node(t), :] = s.keep[t : t + 1, :] * (
-                here_top
-                + jnp.where(
-                    lane_col == ELY - 1, turned(high_all, ELY - 1 - k), turned(here_bottom, -1)
-                )
+                here_top + jnp.where(lane_col == ELY - 1, ends, turned(here_bottom, -1))
             )
         for _, leave in copies:
             leave()
@@ -682,10 +752,11 @@
             precision=HIGHEST,
             preferred_element_type=jnp.float32,
         )
-        s.ps[turn] = total[0:1, :]
+        for k in range(p.peers):
+            s.ps[turn, k] = total[0:1, :]
         copies = [
             remote(
-                s.ps.at[turn], s.pr.at[turn, k], s.s_sum, (turn, k),
+                s.ps.at[turn, k], s.pr.at[turn, k], s.s_sum, (turn,),
                 {"ex": shifted("ex", a), "ey": shifted("ey", b)},
             )
             for k, (a, b) in enumerate(around)
@@ -695,12 +766,15 @@
         return copies
 
     def sums_end(turn, copies):
-        total = s.ps[turn]
-        for k, copy in enumerate(copies):
-            copy.wait_recv()
+        whole = remote(
+            s.ps.at[turn], s.pr.at[turn], s.s_sum, (turn,),
+            {"ex": shifted("ex", around[0][0]), "ey": shifted("ey", around[0][1])},
+        )
+        whole.wait_recv()
+        total = s.ps[turn, 0]
+        for k in range(p.peers):
             total = total + s.pr[turn, k]
-        for copy in copies:
-            copy.wait_send()
+        whole.wait_send()
         row = lax.broadcasted_iota(jnp.int32, (m, 2 * m), 0)
         column = lax.broadcasted_iota(jnp.int32, (m, 2 * m), 1)
         pick = lambda offset: jnp.sum(
@@ -717,16 +791,16 @@
             s.res[rows, :] = s.res[rows, :] + spread(arrived, n, mc, False)
 
     def add_far(piece):
-        def one_node(i):
-            n = bounds[piece] + i
-            rows = tile((NB + n) * gp, gm)
-            total = s.spec[rows, :]
+        def some_nodes(nodes):
+            totals = [s.spec[tile((NB + n) * gp, gm), :] for n in nodes]
             for g in hops:
-                total = total + dot(s.fwd[g], pile(s.fo[g - 1, n]))
-            s.spec[rows, :] = total
+                more = apply_table(s.fwd[g], [s.fo[g - 1, n] for n in nodes])
+                totals = [total + value for total, value in zip(totals, more)]
+            for n, total in zip(nodes, totals):
+                s.spec[tile((NB + n) * gp, gm), :] = total
 
         arrive(second[piece])
-        loop(bounds[piece + 1] - bounds[piece], 7, one_node)
+        pairs(bounds[piece], bounds[piece + 1], 4, some_nodes)
 
     assemble(s.res, 0, lambda: add_far(0))
 
@@ -735,9 +809,9 @@
         operator()
         copies = sums_start(turn)
         if turn < ITERS - 1:
-            assemble(s.app, turn + 1, (lambda: add_far(1)) if turn else (lambda: None))
+            assemble(s.app, turn + 1, fillers[turn])
         else:
-            add_far(2)
+            add_far(1)
         norm, curve = sums_end(turn, copies)
         if turn == 0:
             step_size = norm / curve
@@ -788,68 +862,77 @@
     for _, _, copy in first:
         copy.wait_send()
 
-    for piece in range(3, len(second)):
+    for piece in range(2, len(second)):
         add_far(piece)
     inverse_coef = 1.0 / s.coef[...]
 
     def restore(g, c, load):
-        per = LANES // mo
+        per = WIDE // mo
         for block in range(NB // per):
             nodes = range(block * per, (block + 1) * per)
             rows = permuted(jnp.concatenate([load(n) for n in nodes], 0), s.oneT)
             for k, n in enumerate(nodes):
-                piece = rows[k * mo : (k + 1) * mo]
-                s.xe[n * op : n * op + mo, :] = piece
                 start_row = n * gp + g * m + c * mo
-                s.spec[start_row : start_row + mo, :] = piece
-
-    def from_inner(j):
-        inner = s.spec[pl.ds(NB * gp + j, DEEP, stride=gp), :]
-        matrix = s.invf[tile(j * TALL, TALL), :DEEP]
-        return product(matrix, inner) * inverse_coef
-
-    def from_cycle(j, k):
-        matrix = s.ct[tile(j * DEEP, TALL), :NB]
-        return product(matrix, s.xe[pl.ds(k, NB, stride=op), :])
-
-    def inner_rows(j):
-        return pl.ds(NB * gp + j, NI, stride=gp)
+                s.spec[start_row : start_row + mo, :] = rows[k * mo : (k + 1) * mo]
+
+    def inner_rows(j, count):
+        return pl.ds(NB * gp + j, count, stride=gp)
+
+    def matrix(j, lanes):
+        return s.invf[tile(j * TALL, TALL), lanes]
+
+    def scaled(j):
+        return s.spec[inner_rows(j, DEEP), :] * inverse_coef
+
+    def cycle(j):
+        return s.spec[pl.ds(j, NB, stride=gp), :]
+
+    def whole_mode(j):
+        both = jnp.concatenate([scaled(j), cycle(j)], 0)
+        s.spec[inner_rows(j, NI), :] = product(matrix(j, pl.ds(0, DEEP + NB)), both)[:NI]
+
+    def base(j):
+        s.spec[inner_rows(j, NI), :] = product(matrix(j, pl.ds(0, DEEP)), scaled(j))[:NI]
+
+    def correct(j):
+        value = product(matrix(j, pl.ds(DEEP, NB)), cycle(j))
+        s.spec[inner_rows(j, NI), :] = s.spec[inner_rows(j, NI), :] + value[:NI]
 
     for c in range(p.parts):
         restore(0, c, solved(c))
-
-        def own_mode(k, c=c):
-            j = c * mo + k
-            s.spec[inner_rows(j), :] = (from_inner(j) - from_cycle(j, k))[:NI]
-
-        loop(mo, 8, own_mode)
-
-    def own_velocity(n):
-        out[n] = dot(s.back[...], pile(s.spec[tile(n * gp, m), :]))
-
-    loop(NODES, 9, own_velocity)
-
-    def base(k):
-        s.spec[inner_rows(m + k), :] = from_inner(m + k)[:NI]
-
-    loop(gm - m, 8, base)
+        loop(mo, 16, lambda k, c=c: whole_mode(c * mo + k))
+
+    def own_velocity(nodes):
+        rows = [s.spec[tile(n * gp, m), :] for n in nodes]
+        for n, value in zip(nodes, apply_table(s.back[...], rows)):
+            out[n] = value
+
+    pairs(0, NODES, 4, own_velocity)
+
+    late = gm - mo
+    loop(mo, 16, lambda k: base(late + k))
 
     for g, c, copy in third:
         copy.wait_recv()
         arrived = planes_of(s.xr.at[g - 1, c], mo)
         restore(g, c, lambda n, arrived=arrived: spread(arrived, n, mo, True))
-
-        def far_mode(k, g=g, c=c):
-            j = g * m + c * mo + k
-            s.spec[inner_rows(j), :] = s.spec[inner_rows(j), :] - from_cycle(j, k)[:NI]
-
-        loop(mo, 8, far_mode)
-
-        def far_velocity(n, g=g, c=c):
-            rows = s.spec[tile(n * gp + g * m + c * mo, mo), :]
-            out[n] = out[n] + dot(s.far[(g - 1) * p.parts + c], pile(rows))
-
-        loop(NODES, 9, far_velocity)
+        first_mode = g * m + c * mo
+
+        def far_mode(k, first_mode=first_mode):
+            if first_mode == late:
+                correct(first_mode + k)
+            else:
+                whole_mode(first_mode + k)
+
+        loop(mo, 16, far_mode)
+
+        def far_velocity(nodes, g=g, c=c, first_mode=first_mode):
+            rows = [s.spec[tile(n * gp + first_mode, mo), :] for n in nodes]
+            values = apply_table(s.far[(g - 1) * p.parts + c], rows)
+            for n, value in zip(nodes, values):
+                out[n] = out[n] + value
+
+        pairs(0, NODES, 4, far_velocity)
 
     for _, _, copy in third:
         copy.wait_send()

time: 80.8 us -> 78.4 us (0.970)
  Pallas kernels: 78.1 us -> 76.2 us
    pallas_call x1, Pallas kernels: 78.1 us -> 76.2 us  [on_device(): pl.pallas_call(functools.partial(kernel, p, tuple(scratch)), out_shape=ja...]
where the time goes in v3:
time: 78.4 us; the launch traced here: 78.2 us
  Pallas kernels  76.2 us (97%)
  local copies, waits for them, and re-layouts  1.5 us (2%)
    pallas_call x1, Pallas kernels, on_device(): pl.pallas_call(functools.partial(kernel, p, tuple(scratch)), out_shape=ja...  76.2 us

profile of v3, /device:TPU:0, one launch (start us, length us, event | category | flops | bytes accessed | tf_op | source)
XLA Modules:
  0.0 78.2 jit_solution(8799117012446412082)
XLA Ops:
  0.0 0.5 select_select_fusion.table
  0.5 76.2 %shard_map.64 = f32[81,64,128]{2,1,0:T(8,128)S(1)} custom-call(f32[81,64,128]{2,1,0:T(8,128)} %bitcast.8, f32[1,128]{1,0:T(1,128)} %bitcast.12, s32[1,128]{1,0:T(1,128)} %bitcast.13, f32[32,32,64]{2,1,0:T(8,128)} %bitcast.11, f32[49,32,64]{2,1,0:T(8,128)} %bitcast.10, f32[49,49,64]{2,1,0:T(8,128)} %bitcast.9, f32[128,128]{1,0:T(8,128)S(1)} %select_select_fusion.table), custom_call_target="tpu_custom_call" | custom-call | flops 1000000000 | bytes 200000000 | tf_op jit(solution)/shard_map/pallas_call | solution.py:958
  76.7 1.5 %copy.8 = f32[64,81,128]{2,0,1:T(8,128)} copy(f32[64,81,128]{2,0,1:T(8,128)S(1)} %bitcast.7) | data formatting | bytes 5308416
  (3 shorter events, 0.0 us)

commit v4 on v3

--- a/solution.py
+++ b/solution.py
@@ -322,15 +322,10 @@
         if stop > start:
             ref[pl.ds(start, stop - start), :] = jnp.zeros((stop - start, LANES), jnp.float32)
 
-    for g in range(p.groups):
-        s.fwd[g] = stacked(table[:, g * z : (g + 1) * z])
-
     br = p.couple_rows
     own_rows = NI * br
     got_rows = p.couple_part * p.couple_ways
-    clear(s.cpack.at[0], own_rows, p.couple_all)
-    for g in hops:
-        clear(s.cpack.at[g], got_rows, p.couple_all)
+    clear(s.cpack.at[0], own_rows, got_rows)
     loads[0].wait()
     for i in range(NI):
         s.cpack[0, i * br : (i + 1) * br, :] = jnp.concatenate(
@@ -403,14 +398,22 @@
     second = [
         [
             remote(
-                forcing.at[pl.ds(NB + a, b - a)], s.fo.at[g - 1, pl.ds(a, b - a)], s.s_f2,
+                s.f.at[pl.ds(NB + a, b - a)], s.fo.at[g - 1, pl.ds(a, b - a)], s.s_f2,
                 (g - 1, k), {"fourier": shifted("fourier", g)},
             )
             for g in hops
         ]
         for k, (a, b) in enumerate(zip(bounds, bounds[1:]))
     ]
+    loads[2].wait()
     start(second[0])
+
+    clear(s.cpack.at[0], got_rows, p.couple_all)
+    for g in hops:
+        clear(s.cpack.at[g], got_rows, p.couple_all)
+
+    for g in range(p.groups):
+        s.fwd[g] = stacked(table[:, g * z : (g + 1) * z])
 
     def flat(pack, g, start, count, stride, width):
         rows = pack[g, pl.ds(start, count, stride=stride) if stride > 1 else pl.ds(start, count), :]
@@ -441,7 +444,6 @@
             s.spec[tile(n * gp, gm), :] = value
 
     clear(s.spec, NODES * gp, (NB + DEEP) * gp)
-    loads[2].wait()
     pairs(NB, NODES, 4, spectrum)
     loads[3].wait()
     pairs(0, NB, 4, spectrum)

time: 78.4 us -> 78.4 us (level)
  no operation moved by 1% of the time
where the time goes in v4:
time: 78.4 us; the launch traced here: 78.2 us
  Pallas kernels  76.2 us (97%)
  local copies, waits for them, and re-layouts  1.5 us (2%)
    pallas_call x1, Pallas kernels, on_device(): pl.pallas_call(functools.partial(kernel, p, tuple(scratch)), out_shape=ja...  76.2 us

profile of v4, /device:TPU:0, one launch (start us, length us, event | category | flops | bytes accessed | tf_op | source)
XLA Modules:
  0.0 78.2 jit_solution(2466517742555575898)
XLA Ops:
  0.0 0.5 select_select_fusion.table
  0.5 76.2 %shard_map.64 = f32[81,64,128]{2,1,0:T(8,128)S(1)} custom-call(f32[81,64,128]{2,1,0:T(8,128)} %bitcast.8, f32[1,128]{1,0:T(1,128)} %bitcast.12, s32[1,128]{1,0:T(1,128)} %bitcast.13, f32[32,32,64]{2,1,0:T(8,128)} %bitcast.11, f32[49,32,64]{2,1,0:T(8,128)} %bitcast.10, f32[49,49,64]{2,1,0:T(8,128)} %bitcast.9, f32[128,128]{1,0:T(8,128)S(1)} %select_select_fusion.table), custom_call_target="tpu_custom_call" | custom-call | flops 1000000000 | bytes 200000000 | tf_op jit(solution)/shard_map/pallas_call | solution.py:960
  76.7 1.5 %copy.8 = f32[64,81,128]{2,0,1:T(8,128)} copy(f32[64,81,128]{2,0,1:T(8,128)S(1)} %bitcast.7) | data formatting | bytes 5308416
  (3 shorter events, 0.0 us)
